TPU v7x, 32 devices: a whole 2x2x4 slice. The times are simulated.
32 devices in a mesh: rep: 4 (over x, y), dp: 8 (over z, core).
Axes of the slice: x: 2, y: 2, z: 4, core: 2. Of those that a mesh axis runs over, the one named last changes fastest.
Arguments:
- x: bfloat16 [32, 2048, 768], P(('rep', 'dp')), parts along dimension 0
- dy: bfloat16 [32, 2048, 768], P(('rep', 'dp')), parts along dimension 0
- w_gate: bfloat16 [2, 768, 1792], replicated
- w_up: bfloat16 [2, 768, 1792], replicated
- w_down: bfloat16 [2, 1792, 768], replicated
- m_w_gate: float32 [2, 768, 1792], replicated
- m_w_up: float32 [2, 768, 1792], replicated
- m_w_down: float32 [2, 1792, 768], replicated
- v_w_gate: float32 [2, 768, 1792], replicated
- v_w_up: float32 [2, 768, 1792], replicated
- v_w_down: float32 [2, 1792, 768], replicated
Outputs:
- output 1: bfloat16 [8, 768, 1792], P('rep'), parts along dimension 0
- output 2: bfloat16 [8, 768, 1792], P('rep'), parts along dimension 0
- output 3: bfloat16 [8, 1792, 768], P('rep'), parts along dimension 0
- output 4: float32 [8, 768, 1792], P('rep'), parts along dimension 0
- output 5: float32 [8, 768, 1792], P('rep'), parts along dimension 0
- output 6: float32 [8, 1792, 768], P('rep'), parts along dimension 0
- output 7: float32 [8, 768, 1792], P('rep'), parts along dimension 0
- output 8: float32 [8, 768, 1792], P('rep'), parts along dimension 0
- output 9: float32 [8, 1792, 768], P('rep'), parts along dimension 0
There are 4 independent parts. A program takes and returns all parts, laid end to end along the dimension named above; an argument that names none is the same for every part.
All inputs are finite; a program needn't handle non-finite values.
Results may differ from a plain program's by a relative error of at most 0.022.
Values are sent between devices in bfloat16 or wider.
A program may use at most 2.25 GiB of HBM per device.

v0:
```python
import jax
import jax.numpy as jnp
from jax import lax
from jax.sharding import PartitionSpec as P

NAMES = ("w_gate", "w_up", "w_down")


def matmul(a, w):
    return jnp.dot(a, w, preferred_element_type=jnp.float32).astype(jnp.bfloat16)


def normed(h):
    wide = h.astype(jnp.float32)
    scale = lax.rsqrt(jnp.mean(wide**2, -1, keepdims=True) + 1e-6)
    return (wide * scale).astype(jnp.bfloat16)


def layer(h, w):
    a = normed(h)
    gate = jnp.dot(a, w["w_gate"], preferred_element_type=jnp.float32)
    up = jnp.dot(a, w["w_up"], preferred_element_type=jnp.float32)
    return h + matmul((jax.nn.silu(gate) * up).astype(jnp.bfloat16), w["w_down"])


def adamw(w, m, v, g):
    m = 0.9 * m + 0.1 * g
    v = 0.95 * v + 0.05 * g * g
    step = m * lax.rsqrt(v + 1e-8) + 0.1 * w
    return (w - 0.02 * step).astype(jnp.bfloat16), m, v


def clipped(gradients, sum_of_squares, count):
    factor = jnp.minimum(1.0, 0.5 * lax.rsqrt(sum_of_squares / count + 1e-30))
    return [g * factor for g in gradients]


def solution(mesh):
    def step(x, dy, *arrays):
        weights, m, v = (arrays[i : i + 3] for i in (0, 3, 6))
        layers = weights[0].shape[0]
        h, kept = x[0], []
        for number in range(layers):
            kept.append(h)
            h = layer(h, {name: w[number] for name, w in zip(NAMES, weights, strict=True)})
        by_h, summed = dy[0], [None] * layers
        for number in reversed(range(layers)):
            _, back = jax.vjp(lambda w, h: layer(h, w), {name: w[number] for name, w in zip(NAMES, weights, strict=True)}, kept[number])
            by_w, by_h = back(by_h)
            summed[number] = [lax.psum(by_w[name], "dp") for name in NAMES]
        gradients = [jnp.stack([summed[number][i] for number in range(layers)]).astype(jnp.float32) for i in range(3)]
        gradients = clipped(gradients, sum(jnp.sum(g * g) for g in gradients), sum(g.size for g in gradients))
        new = [adamw(w.astype(jnp.float32), m, v, g) for w, m, v, g in zip(weights, m, v, gradients, strict=True)]
        return tuple(one[which] for which in range(3) for one in new)

    return jax.shard_map(
        step,
        mesh=mesh,
        in_specs=(P(("rep", "dp"), None, None),) * 2 + (P(None, None, None),) * 9,
        out_specs=(P("rep", None, None),) * 9,
        check_vma=False,
    )
```

profile of v0, /device:TPU:0, one launch (start us, length us, event | category | flops | bytes accessed | tf_op | source)
XLA Modules:
  0.0 625.6 jit_solution(6069241695839172071)
XLA Ops:
  7.2 3.2 copy.20
  11.1 5.0 copy.21
  16.2 10.4 %convolution_convert_fusion.1 = bf16[2048,1792]{1,0:T(8,128)(2,1)} fusion(bf16[1,2048,768]{2,1,0:T(8,128)(2,1)} %param.12, bf16[2,1792,768]{2,1,0:T(8,128)(2,1)} %param.15), kind=kOutput, calls=%fused_computation.66 | convolution fusion | flops 5640814592 | bytes 13238272 | tf_op jit(solution)/shard_map/transpose(jvp())/dot_general | solution.py:10
  26.5 11.1 %fusion.77 = f32[2048,1792]{1,0:T(8,128)} fusion(bf16[2,768,1792]{2,1,0:T(8,128)(2,1)} %param.13, bf16[1,2048,768]{2,1,0:T(8,128)(2,1)S(1)} %copy-done.5, f32[2048]{0:T(1024)S(1)} %add_rsqrt_fusion), kind=kOutput, calls=%fused_computation.111 | convolution fusion | flops 5641863168 | bytes 20586496 | tf_op jit(solution)/shard_map/dot_general | solution.py:21
  37.6 16.2 %multiply_convert_fusion.1 = (bf16[2048,1792]{1,0:T(8,128)(2,1)}, f32[2048,1792]{1,0:T(8,128)}) fusion(f32[2048,1792]{1,0:T(8,128)} %fusion.77, bf16[2,768,1792]{2,1,0:T(8,128)(2,1)S(1)} %bitcast.77, bf16[1,2048,768]{2,1,0:T(8,128)(2,1)} %param.11, f32[2048]{0:T(1024)S(1)} %add_rsqrt_fusion), kind=kOutput, calls=%fused_computation.20 | convolution fusion | flops 5663883264 | bytes 42606592 | tf_op jit(solution)/shard_map/dot_general | solution.py:22
  53.9 9.7 %fusion.40 = (f32[2048]{0:T(1024)S(1)}, bf16[2048,768]{0,1:T(8,128)(2,1)S(1)}) fusion(bf16[2048,1792]{1,0:T(8,128)(2,1)} %get-tuple-element.24, bf16[2,1792,768]{2,1,0:T(8,128)(2,1)} %param.15, bf16[1,2048,768]{1,2,0:T(8,128)(2,1)S(1)} %copy.20), kind=kOutput, calls=%fused_computation.73 | convolution fusion | flops 5645006848 | bytes 16392192 | tf_op jit(solution)/shard_map/dot_general | solution.py:10
  65.2 9.3 %fusion.66 = f32[2048,1792]{1,0:T(8,128)} fusion(bf16[2,768,1792]{2,1,0:T(8,128)(2,1)S(1)} %bitcast.77, bf16[2048,768]{0,1:T(8,128)(2,1)S(1)} %get-tuple-element.27, f32[2048]{0:T(1024)S(1)} %fusion.100), kind=kOutput, calls=%fused_computation.100 | convolution fusion | flops 5641863168 | bytes 20586496 | tf_op jit(solution)/shard_map/jvp()/dot_general | solution.py:22
  74.5 23.3 %fusion.2 = (bf16[2048,1792]{1,0:T(8,128)(2,1)}, f32[2048,1792]{1,0:T(8,128)}) fusion(f32[2048,1792]{1,0:T(8,128)} %fusion.66, bf16[2048,1792]{1,0:T(8,128)(2,1)} %convolution_convert_fusion.1, bf16[2,768,1792]{2,1,0:T(8,128)(2,1)} %param.13, bf16[2048,768]{0,1:T(8,128)(2,1)} %copy-done.7, f32[2048]{0:T(1024)S(1)} %fusion.100), kind=kOutput, calls=%fused_computation.11 | convolution fusion | flops 5685903360 | bytes 49946624 | tf_op jit(solution)/shard_map/jvp()/dot_general | solution.py:21
  97.8 10.8 %fusion.57 = bf16[1,768,1792]{2,1,0:T(8,128)(2,1)} fusion(bf16[2048,1792]{1,0:T(8,128)(2,1)} %get-tuple-element.28, bf16[2048,768]{0,1:T(8,128)(2,1)S(1)} %copy-done.8, f32[2048]{0:T(1024)S(1)} %fusion.100), kind=kOutput, calls=%fused_computation.95 | convolution fusion | flops 5641863168 | bytes 13246464 | tf_op jit(solution)/shard_map/transpose(jvp())/dot_general | solution.py:21
  108.6 9.2 %convolution_convert_fusion.4 = bf16[2048,768]{0,1:T(8,128)(2,1)} fusion(bf16[2048,1792]{1,0:T(8,128)(2,1)S(1)} %copy-done.14, bf16[2,768,1792]{2,1,0:T(8,128)(2,1)} %param.13), kind=kOutput, calls=%fused_computation.82 | convolution fusion | flops 5637144576 | bytes 13238272 | tf_op jit(solution)/shard_map/transpose(jvp())/dot_general | solution.py:21
  117.8 14.1 %fusion.61 = bf16[1,1792,768]{2,1,0:T(8,128)(2,1)} fusion(bf16[1,2048,768]{2,1,0:T(8,128)(2,1)S(1)} %copy-done.6, f32[2048,1792]{1,0:T(8,128)} %fusion.66, f32[2048,1792]{1,0:T(8,128)} %get-tuple-element.29), kind=kOutput, calls=%fused_computation.99 | convolution fusion | flops 5660540928 | bytes 35258368 | tf_op jit(solution)/shard_map/transpose(jvp())/dot_general | solution.py:10
  131.9 12.5 %fusion.60 = bf16[1,768,1792]{2,1,0:T(8,128)(2,1)} fusion(bf16[2048,1792]{1,0:T(8,128)(2,1)} %convolution_convert_fusion.1, bf16[2048,768]{0,1:T(8,128)(2,1)S(1)} %copy-done.9, f32[2048]{0:T(1024)S(1)} %fusion.100, f32[2048,1792]{1,0:T(8,128)} %get-tuple-element.29), kind=kOutput, calls=%fused_computation.98 | convolution fusion | flops 5665259520 | bytes 27926528 | tf_op jit(solution)/shard_map/transpose(jvp())/dot_general | solution.py:22
  144.4 14.0 %fusion.42 = (f32[2048]{0:T(1024)S(1)}, bf16[2048,768]{0,1:T(8,128)(2,1)}) fusion(bf16[2048,768]{0,1:T(8,128)(2,1)} %copy-done.7, bf16[2048,768]{0,1:T(8,128)(2,1)} %convolution_convert_fusion.4, bf16[2,768,1792]{2,1,0:T(8,128)(2,1)S(1)} %bitcast.79, bf16[2048,1792]{1,0:T(8,128)(2,1)} %convolution_convert_fusion.1, f32[2048,1792]{1,0:T(8,128)} %get-tuple-element.29), kind=kOutput, calls=%fused_computation.75 | convolution fusion | flops 5668599808 | bytes 34217984 | tf_op jit(solution)/shard_map/transpose(jvp())/dot_general | solution.py:22
  158.5 5.2 fusion.51
  163.6 9.4 %fusion.58 = bf16[1,1792,768]{2,1,0:T(8,128)(2,1)} fusion(bf16[2048,1792]{1,0:T(8,128)(2,1)} %get-tuple-element.24, bf16[2048,768]{0,1:T(8,128)(2,1)S(1)} %fusion.51), kind=kOutput, calls=%fused_computation.96 | convolution fusion | flops 5638520832 | bytes 13238272 | tf_op jit(solution)/shard_map/transpose(jvp())/dot_general | solution.py:10
  173.1 6.4 %convolution_convert_fusion = bf16[2048,1792]{1,0:T(8,128)(2,1)S(1)} fusion(bf16[2048,768]{0,1:T(8,128)(2,1)S(1)} %fusion.51, bf16[2,1792,768]{2,1,0:T(8,128)(2,1)S(1)} %bitcast.81), kind=kOutput, calls=%fused_computation.65 | convolution fusion | flops 5640814592 | bytes 13238272 | tf_op jit(solution)/shard_map/transpose(jvp())/dot_general | solution.py:10
  179.5 14.2 %fusion.59 = bf16[1,768,1792]{2,1,0:T(8,128)(2,1)} fusion(bf16[2048,1792]{1,0:T(8,128)(2,1)S(1)} %convolution_convert_fusion, bf16[1,2048,768]{1,2,0:T(8,128)(2,1)S(1)} %copy-done.1, f32[2048]{0:T(1024)S(1)} %copy-done.13, f32[2048,1792]{1,0:T(8,128)} %fusion.77), kind=kOutput, calls=%fused_computation.97 | convolution fusion | flops 5665259520 | bytes 27926528 | tf_op jit(solution)/shard_map/transpose(jvp())/dot_general | solution.py:22
  193.7 17.0 %fusion.54 = bf16[1,768,1792]{2,1,0:T(8,128)(2,1)} fusion(f32[2048,1792]{1,0:T(8,128)} %fusion.77, f32[2048,1792]{1,0:T(8,128)} %get-tuple-element.25, bf16[2048,1792]{1,0:T(8,128)(2,1)} %copy-done.15, bf16[1,2048,768]{1,2,0:T(8,128)(2,1)S(1)} %copy-done.1, f32[2048]{0:T(1024)S(1)} %copy-done.13), kind=kOutput, calls=%fused_computation.94 | convolution fusion | flops 5683609600 | bytes 42606592 | tf_op jit(solution)/shard_map/transpose(jvp())/dot_general | solution.py:21
  210.7 330.7 %all-reduce.3.cloned.1.call-done = (bf16[1,768,1792]{2,1,0:T(8,128)(2,1)}, bf16[1,768,1792]{2,1,0:T(8,128)(2,1)}, bf16[1,768,1792]{2,1,0:T(8,128)(2,1)}, bf16[1,...) async-done(((bf16[1,768,1792]{2,1,0:T(8,128)(2,1)}, bf16[1,768,1792]{2,1,0:T(8,128)(2,1)}, bf16[1,768,1792]{2,1,0:T(8,128)(2,1)}, ...) | async-done | bytes 16515088 | tf_op jit(solution)/shard_map/psum | solution.py:50
  541.4 6.2 fusion.22
  547.6 6.0 fusion.21
  553.7 3.4 fusion.20
  559.1 21.9 %fusion.28 = (bf16[2,1792,768]{2,1,0:T(8,128)(2,1)}, f32[2,1792,768]{2,1,0:T(8,128)}, f32[2,1792,768]{2,1,0:T(8,128)}) fusion(bf16[2,1792,768]{2,1,0:T(8,128)(2,1)} %param.15, f32[]{:T(128)S(6)} %min_shard_map.3, bf16[1,1792,768]{2,1,0:T(8,128)(2,1)} %get-tuple-element.13, bf16[1,1792,768]{2,1,0:T(8,128)(2,1)} %get-tuple-element.14, ...), kind=kLoop, calls=%fused_computation.52 | loop fusion | flops 55050240 | bytes 60555268 | tf_op jit(solution)/shard_map/convert_element_type | solution.py:30
  581.0 37.3 %fusion.19 = (bf16[2,768,1792]{2,1,0:T(8,128)(2,1)}, f32[2,768,1792]{2,1,0:T(8,128)}, f32[2,768,1792]{2,1,0:T(8,128)}, bf16[2,768,1792]{2,1,0:T(8,128)(2,1)}, f3...) fusion(bf16[2,768,1792]{2,1,0:T(8,128)(2,1)} %param.13, f32[]{:T(128)S(6)} %min_shard_map.3, ...), kind=kLoop, calls=%fused_computation.43 | loop fusion | flops 110100480 | bytes 121110528 | tf_op jit(solution)/shard_map/convert_element_type | solution.py:30
  (53 shorter events, 2.5 us)
Async XLA Ops:
  7.2 534.2 %all-reduce.3.cloned.1.call-start = ((), (), s32[]{:S(2)}) async-start(), calls=%async_computation | async-start | bytes 33030144 | tf_op jit(solution)/shard_map/psum | solution.py:50
  10.4 43.4 %copy-start = (bf16[1,2048,768]{1,2,0:T(8,128)(2,1)}, bf16[1,2048,768]{1,2,0:T(8,128)(2,1)S(1)}, u32[]{:S(2)}) copy-start(bf16[1,2048,768]{1,2,0:T(8,128)(2,1)S(1)} %copy.20) | copy-start | bytes 9437188
  11.1 26.5 %copy-start.12 = (f32[2048]{0:T(1024)}, f32[2048]{0:T(1024)S(1)}, u32[]{:S(2)}) copy-start(f32[2048]{0:T(1024)S(1)} %add_rsqrt_fusion) | copy-start | bytes 24580
  16.1 10.4 %copy-start.5 = (bf16[1,2048,768]{2,1,0:T(8,128)(2,1)S(1)}, bf16[1,2048,768]{2,1,0:T(8,128)(2,1)}, u32[]{:S(2)}) copy-start(bf16[1,2048,768]{2,1,0:T(8,128)(2,1)} %param.11) | copy-start | bytes 9437188
  16.1 21.4 %slice-start = ((s8[5505024]{0:T(1024)(128)(4,1)}), s8[4194304]{0:T(1024)(128)(4,1)S(1)}, s32[]{:S(2)}) async-start(s8[5505024]{0:T(1024)(128)(4,1)} %bitcast.76), calls=%async_computation.1 | async-start | bytes 8388608
  26.5 11.1 %slice-start.1 = ((s8[5505024]{0:T(1024)(128)(4,1)}), s8[1310720]{0:T(1024)(128)(4,1)S(1)}, s32[]{:S(2)}) async-start(s8[5505024]{0:T(1024)(128)(4,1)} %bitcast.76), calls=%async_computation.2 | async-start | bytes 2621440
  63.5 1.7 copy-start.7
  63.5 1.7 copy-start.10
  74.5 23.3 %copy-start.8 = (bf16[2048,768]{0,1:T(8,128)(2,1)S(1)}, bf16[2048,768]{0,1:T(8,128)(2,1)}, u32[]{:S(2)}) copy-start(bf16[2048,768]{0,1:T(8,128)(2,1)} %copy-done.7) | copy-start | bytes 9437188
  97.8 10.8 %copy-start.14 = (bf16[2048,1792]{1,0:T(8,128)(2,1)S(1)}, bf16[2048,1792]{1,0:T(8,128)(2,1)}, u32[]{:S(2)}) copy-start(bf16[2048,1792]{1,0:T(8,128)(2,1)} %get-tuple-element.28) | copy-start | bytes 22020100
  108.6 9.2 %copy-start.6 = (bf16[1,2048,768]{2,1,0:T(8,128)(2,1)S(1)}, bf16[1,2048,768]{2,1,0:T(8,128)(2,1)}, u32[]{:S(2)}) copy-start(bf16[1,2048,768]{2,1,0:T(8,128)(2,1)} %param.12) | copy-start | bytes 9437188
  117.8 14.1 %copy-start.9 = (bf16[2048,768]{0,1:T(8,128)(2,1)S(1)}, bf16[2048,768]{0,1:T(8,128)(2,1)}, u32[]{:S(2)}) copy-start(bf16[2048,768]{0,1:T(8,128)(2,1)} %copy-done.7) | copy-start | bytes 9437188
  117.8 26.6 %slice-start.2 = ((s8[5505024]{0:T(1024)(128)(4,1)}), s8[4194304]{0:T(1024)(128)(4,1)S(1)}, s32[]{:S(2)}) async-start(s8[5505024]{0:T(1024)(128)(4,1)} %bitcast.78), calls=%async_computation.3 | async-start | bytes 8388608
  131.9 12.5 %slice-start.3 = ((s8[5505024]{0:T(1024)(128)(4,1)}), s8[1310720]{0:T(1024)(128)(4,1)S(1)}, s32[]{:S(2)}) async-start(s8[5505024]{0:T(1024)(128)(4,1)} %bitcast.78), calls=%async_computation.4 | async-start | bytes 2621440
  144.4 14.0 %copy-start.11 = (f32[2048]{0:T(1024)S(1)}, f32[2048]{0:T(1024)}, u32[]{:S(2)}) copy-start(f32[2048]{0:T(1024)} %copy-done.10) | copy-start | bytes 24580
  144.4 14.0 %copy-start.2 = (bf16[1,2048,768]{1,2,0:T(8,128)(2,1)S(1)}, bf16[1,2048,768]{1,2,0:T(8,128)(2,1)}, u32[]{:S(2)}) copy-start(bf16[1,2048,768]{1,2,0:T(8,128)(2,1)} %copy.21) | copy-start | bytes 9437188
  158.4 14.6 %slice-start.4 = ((s8[5505024]{0:T(1024)(128)(4,1)}), s8[1310720]{0:T(1024)(128)(4,1)S(1)}, s32[]{:S(2)}) async-start(s8[5505024]{0:T(1024)(128)(4,1)} %bitcast.80), calls=%async_computation.5 | async-start | bytes 2621440
  163.6 9.4 %slice-start.5 = ((s8[5505024]{0:T(1024)(128)(4,1)}), s8[4194304]{0:T(1024)(128)(4,1)S(1)}, s32[]{:S(2)}) async-start(s8[5505024]{0:T(1024)(128)(4,1)} %bitcast.80), calls=%async_computation.6 | async-start | bytes 8388608
  173.0 6.4 %copy-start.1 = (bf16[1,2048,768]{1,2,0:T(8,128)(2,1)S(1)}, bf16[1,2048,768]{1,2,0:T(8,128)(2,1)}, u32[]{:S(2)}) copy-start(bf16[1,2048,768]{1,2,0:T(8,128)(2,1)} %copy-done) | copy-start | bytes 9437188
  173.0 6.4 %copy-start.13 = (f32[2048]{0:T(1024)S(1)}, f32[2048]{0:T(1024)}, u32[]{:S(2)}) copy-start(f32[2048]{0:T(1024)} %copy-done.12) | copy-start | bytes 24580
  179.5 14.2 %copy-start.15 = (bf16[2048,1792]{1,0:T(8,128)(2,1)}, bf16[2048,1792]{1,0:T(8,128)(2,1)S(1)}, u32[]{:S(2)}) copy-start(bf16[2048,1792]{1,0:T(8,128)(2,1)S(1)} %convolution_convert_fusion) | copy-start | bytes 22020100
  541.4 12.2 %copy-start.3 = (bf16[1,768,1792]{2,1,0:T(8,128)(2,1)S(1)}, bf16[1,768,1792]{2,1,0:T(8,128)(2,1)}, u32[]{:S(2)}) copy-start(bf16[1,768,1792]{2,1,0:T(8,128)(2,1)} %get-tuple-element.9) | copy-start | bytes 8257540
  541.4 12.2 %copy-start.4 = (bf16[1,768,1792]{2,1,0:T(8,128)(2,1)S(1)}, bf16[1,768,1792]{2,1,0:T(8,128)(2,1)}, u32[]{:S(2)}) copy-start(bf16[1,768,1792]{2,1,0:T(8,128)(2,1)} %get-tuple-element.10) | copy-start | bytes 8257540
Sparse Core Ops, SparseCore 0:
  210.8 330.5 all-reduce.2
where the time goes:
time: 633 us; the launch traced here: 626 us
  waiting for transfers between devices  331 us (52%)
  matrix products  187 us (30%)
  other arithmetic  80.7 us (13%)
  between operations  16.7 us (3%)
  local copies, waits for them, and re-layouts  9.95 us (2%)
    psum x1, waiting for transfers between devices, step(): summed[number] = [lax.psum(by_w[name], 'dp') for name in NAMES]  331 us
    dot_general x5, matrix products, layer(): gate = jnp.dot(a, w['w_gate'], preferred_element_type=jnp.float32)  71.4 us
    dot_general x5, matrix products, layer(): up = jnp.dot(a, w['w_up'], preferred_element_type=jnp.float32)  66.2 us
    convert_element_type x2, other arithmetic, adamw(): return ((w - 0.02 * step).astype(jnp.bfloat16), m, v)  59.2 us
    dot_general x5, matrix products, matmul(): jnp.dot(a, w, preferred_element_type=jnp.float32).astype(jnp.bfloat16)  50 us
    reduce_sum x3, other arithmetic, step(): jnp.sum(g * g)  15.7 us
  transfers between devices with their start and end apart: 1, of which 1 were waited for; matrix products, arithmetic and copies ran while one was open for 0% of the time, Pallas kernels for 0%

commit v1 on v0

--- a/solution.py
+++ b/solution.py
@@ -1,6 +1,8 @@
 import jax
 import jax.numpy as jnp
 from jax import lax
+from jax.experimental import pallas as pl
+from jax.experimental.pallas import tpu as pltpu
 from jax.sharding import PartitionSpec as P
 
 NAMES = ("w_gate", "w_up", "w_down")
@@ -33,6 +35,230 @@
 def clipped(gradients, sum_of_squares, count):
     factor = jnp.minimum(1.0, 0.5 * lax.rsqrt(sum_of_squares / count + 1e-30))
     return [g * factor for g in gradients]
+
+
+MESH = pl.DeviceIdType.MESH
+MATS = 6
+ROWS, COLS = 768, 1792
+HALF, QUARTER = ROWS // 2, ROWS // 4
+SUB = 4
+PIECE = QUARTER // SUB
+N = MATS * SUB
+SKEW = 2
+LINE = 4
+
+
+def place(q):
+    return lax.rem(lax.rem(q, 3) + 2, 3) * 2 + 1 - q // 3
+
+
+def sum_kernel(*refs):
+    terms = refs[:MATS]
+    out, squares_out, t, p, r, acc, tile, sq, load, xs, xr, right_s, left_s, rs_r, ag_r, d_s, d_r, out_s, sq_s, sq_r = refs[MATS:]
+    dp = lax.axis_index("dp")
+    z, c = dp // 2, lax.rem(dp, 2)
+    other = z * 2 + 1 - c
+
+    loads = [pltpu.make_async_copy(terms[m], t.at[pl.ds(m * ROWS, ROWS)], load.at[m]) for m in range(MATS)]
+    order = [4 + 1, 0 + 1, 2 + 1, 4, 0, 2]
+    for m in order:
+        loads[m].start()
+    barrier = pltpu.get_barrier_semaphore()
+    for step in range(1, 8):
+        pl.semaphore_signal(barrier, inc=1, device_id={"dp": lax.rem(dp + step, 8)}, device_id_type=MESH)
+    pl.semaphore_wait(barrier, 7)
+    acc[...] = jnp.zeros_like(acc)
+
+    def exchange(m, x):
+        return pltpu.make_async_remote_copy(
+            src_ref=t.at[pl.ds(pl.multiple_of(m * ROWS + (1 - c) * HALF + x * QUARTER, 16), QUARTER)],
+            dst_ref=p.at[pl.ds(pl.multiple_of(m * HALF + x * QUARTER, 16), QUARTER)],
+            send_sem=xs,
+            recv_sem=xr.at[x * MATS + m],
+            device_id={"dp": other},
+            device_id_type=MESH,
+        )
+
+    for m in order:
+        loads[m].wait()
+        for x in range(2):
+            exchange(m, x).start()
+
+    def wide(k, x, core):
+        m = place(k // SUB)
+        return pl.ds(pl.multiple_of(m * ROWS + core * HALF + x * QUARTER + lax.rem(k, SUB) * PIECE, 16), PIECE)
+
+    def narrow(k, x):
+        m = place(k // SUB)
+        return pl.ds(pl.multiple_of(m * HALF + x * QUARTER + lax.rem(k, SUB) * PIECE, 16), PIECE)
+
+    def sum_copy(k, x):
+        return pltpu.make_async_remote_copy(
+            src_ref=p.at[narrow(k, x)],
+            dst_ref=r.at[narrow(k, x)],
+            send_sem=right_s if x == 0 else left_s,
+            recv_sem=rs_r.at[x * N + k],
+            device_id={"dp": dp + 2 if x == 0 else dp - 2},
+            device_id_type=MESH,
+        )
+
+    def back_copy(k, x, first=False):
+        return pltpu.make_async_remote_copy(
+            src_ref=r.at[narrow(k, x)] if first else out.at[wide(k, x, c)],
+            dst_ref=out.at[wide(k, x, c)],
+            send_sem=left_s if x == 0 else right_s,
+            recv_sem=ag_r.at[x * N + k],
+            device_id={"dp": dp - 2 if x == 0 else dp + 2},
+            device_id_type=MESH,
+        )
+
+    def share_copy(k, x, first=False):
+        return pltpu.make_async_remote_copy(
+            src_ref=r.at[narrow(k, x)] if first else out.at[wide(k, x, c)],
+            dst_ref=out.at[wide(k, x, c)],
+            send_sem=d_s,
+            recv_sem=d_r.at[x * N + k],
+            device_id={"dp": other},
+            device_id_type=MESH,
+        )
+
+    def share_arrival(k, x):
+        return pltpu.make_async_remote_copy(
+            src_ref=out.at[wide(k, x, 1 - c)],
+            dst_ref=out.at[wide(k, x, 1 - c)],
+            send_sem=d_s,
+            recv_sem=d_r.at[x * N + k],
+            device_id={"dp": other},
+            device_id_type=MESH,
+        )
+
+    def valid(k):
+        return jnp.logical_and(k >= 0, k < N)
+
+    def add(k, x):
+        hops = z if x == 0 else LINE - 1 - z
+
+        @pl.when(lax.rem(k, SUB) == 0)
+        def _():
+            exchange(place(k // SUB), x).wait_recv()
+
+        mine = t[wide(k, x, c), :].astype(jnp.float32) + p[narrow(k, x), :].astype(jnp.float32)
+
+        @pl.when(hops == 0)
+        def _():
+            p[narrow(k, x), :] = mine.astype(jnp.bfloat16)
+            sum_copy(k, x).start()
+
+        @pl.when(hops > 0)
+        def _():
+            sum_copy(k, x).wait_recv()
+            mine = t[wide(k, x, c), :].astype(jnp.float32) + p[narrow(k, x), :].astype(jnp.float32)
+            total = (mine + r[narrow(k, x), :].astype(jnp.float32)).astype(jnp.bfloat16)
+
+            @pl.when(hops < LINE - 1)
+            def _():
+                p[narrow(k, x), :] = total
+                sum_copy(k, x).start()
+
+            @pl.when(hops == LINE - 1)
+            def _():
+                r[narrow(k, x), :] = total
+                back_copy(k, x, True).start()
+                share_copy(k, x, True).start()
+                pltpu.make_async_copy(r.at[narrow(k, x)], out.at[wide(k, x, c)], out_s).start()
+                g = total.astype(jnp.float32)
+                acc[...] += jnp.sum((g * g).reshape(PIECE // 8, 8, COLS), axis=0)
+
+    def relay(k, x):
+        back_copy(k, x).wait_recv()
+
+        @pl.when((z if x == 0 else LINE - 1 - z) > 0)
+        def _():
+            back_copy(k, x).start()
+
+        share_copy(k, x).start()
+
+    turn = SKEW * (LINE - 1)
+
+    @pl.loop(0, N + 2 * turn + 1)
+    def _(i):
+        for x in range(2):
+            k = i - SKEW * (z if x == 0 else LINE - 1 - z)
+            pl.when(valid(k))(lambda k=k, x=x: add(k, x))
+        for x in range(2):
+            back = LINE - 1 - z if x == 0 else z
+            k = i - turn - SKEW * back
+            pl.when(jnp.logical_and(back > 0, valid(k)))(lambda k=k, x=x: relay(k, x))
+            k = k - 1
+
+            @pl.when(valid(k))
+            def _(k=k, x=x):
+                share_arrival(k, x).wait_recv()
+
+    total = jnp.sum(acc[...])
+    tile[...] = jnp.full(tile.shape, total, jnp.float32)
+
+    def tell(slot, step):
+        return pltpu.make_async_remote_copy(
+            src_ref=tile, dst_ref=sq.at[slot], send_sem=sq_s.at[step - 1], recv_sem=sq_r.at[slot],
+            device_id={"dp": lax.rem(dp + step, 8)}, device_id_type=MESH,
+        )
+
+    for slot, owner in enumerate((0, 1, 6, 7)):
+        @pl.when(dp == owner)
+        def _(slot=slot):
+            for step in range(1, 8):
+                tell(slot, step).start()
+            sq[slot] = tile[...]
+
+        @pl.when(dp != owner)
+        def _(slot=slot):
+            tell(slot, 1).wait_recv()
+
+    squares_out[...] = sq[0] + sq[1] + sq[2] + sq[3]
+
+    for slot, owner in enumerate((0, 1, 6, 7)):
+        @pl.when(dp == owner)
+        def _(slot=slot):
+            for step in range(1, 8):
+                tell(slot, step).wait_send()
+
+    def all_sent(sem):
+        pltpu.make_async_remote_copy(
+            src_ref=p, dst_ref=p, send_sem=sem, recv_sem=xr.at[0], device_id={"dp": other}, device_id_type=MESH
+        ).wait_send()
+
+    pl.when(z < LINE - 1)(lambda: all_sent(right_s))
+    pl.when(z > 0)(lambda: all_sent(left_s))
+    all_sent(d_s)
+    all_sent(xs)
+
+    @pl.when(jnp.logical_or(z == 0, z == LINE - 1))
+    def _():
+        pltpu.make_async_copy(r.at[pl.ds(0, N * PIECE)], out.at[pl.ds(0, N * PIECE)], out_s).wait()
+
+
+def group_sum(terms):
+    dma = pltpu.SemaphoreType.DMA
+    vmem = pltpu.VMEM
+    return pl.pallas_call(
+        sum_kernel,
+        out_shape=(jax.ShapeDtypeStruct((MATS * ROWS, COLS), jnp.bfloat16), jax.ShapeDtypeStruct((8, 128), jnp.float32)),
+        in_specs=[pl.BlockSpec(memory_space=pl.ANY)] * MATS,
+        out_specs=(pl.BlockSpec(memory_space=pl.ANY), pl.BlockSpec(memory_space=pltpu.VMEM)),
+        scratch_shapes=[
+            vmem((MATS * ROWS, COLS), jnp.bfloat16),
+            vmem((MATS * HALF, COLS), jnp.bfloat16),
+            vmem((MATS * HALF, COLS), jnp.bfloat16),
+            vmem((8, COLS), jnp.float32),
+            vmem((8, 128), jnp.float32),
+            vmem((4, 8, 128), jnp.float32),
+            dma((MATS,)), dma(()), dma((2 * MATS,)), dma(()), dma(()), dma((2 * N,)), dma((2 * N,)), dma(()), dma((2 * N,)), dma(()),
+            dma((7,)), dma((4,)),
+        ],
+        compiler_params=pltpu.CompilerParams(collective_id=0, has_side_effects=True, vmem_limit_bytes=60 * 2**20),
+        name="group_sum",
+    )(*terms)
 
 
 def solution(mesh):
@@ -43,13 +269,15 @@
         for number in range(layers):
             kept.append(h)
             h = layer(h, {name: w[number] for name, w in zip(NAMES, weights, strict=True)})
-        by_h, summed = dy[0], [None] * layers
+        by_h, terms = dy[0], [None] * MATS
         for number in reversed(range(layers)):
             _, back = jax.vjp(lambda w, h: layer(h, w), {name: w[number] for name, w in zip(NAMES, weights, strict=True)}, kept[number])
             by_w, by_h = back(by_h)
-            summed[number] = [lax.psum(by_w[name], "dp") for name in NAMES]
-        gradients = [jnp.stack([summed[number][i] for number in range(layers)]).astype(jnp.float32) for i in range(3)]
-        gradients = clipped(gradients, sum(jnp.sum(g * g) for g in gradients), sum(g.size for g in gradients))
+            terms[number], terms[2 + number], terms[4 + number] = by_w["w_gate"], by_w["w_up"], by_w["w_down"].T
+        summed, squares = group_sum(terms)
+        summed = summed.reshape(3, layers, ROWS, COLS)
+        gradients = [summed[0].astype(jnp.float32), summed[1].astype(jnp.float32), summed[2].transpose(0, 2, 1).astype(jnp.float32)]
+        gradients = clipped(gradients, squares[0, 0], sum(g.size for g in gradients))
         new = [adamw(w.astype(jnp.float32), m, v, g) for w, m, v, g in zip(weights, m, v, gradients, strict=True)]
         return tuple(one[which] for which in range(3) for one in new)
 

time: 633 us -> 517 us (0.82)
  waiting for transfers between devices: 331 us -> 0 us
  Pallas kernels: 0 us -> 217 us
  between operations: 16.7 us -> 1.99 us
  local copies, waits for them, and re-layouts: 9.95 us -> 19.7 us
    psum x1 -> x0, waiting for transfers between devices: 331 us -> none  [step(): summed[number] = [lax.psum(by_w[name], 'dp') for name in NAMES]]
    pallas_call x0 -> x1, Pallas kernels: none -> 217 us  [group_sum(): pl.pallas_call(sum_kernel, out_shape=(jax.ShapeDtypeStruct((MATS * ROWS,...]
    reduce_sum x3 -> x0, other arithmetic: 15.7 us -> none  [step(): jnp.sum(g * g)]
    mul x0 -> x1, other arithmetic: none -> 14.4 us  [clipped(): return [g * factor for g in gradients]]
    mul x0 -> x1, local copies, waits for them, and re-layouts: none -> 12.1 us  [clipped(): return [g * factor for g in gradients]]
  transfers between devices with their start and end apart: 1 -> 0, of which waited for: 1 -> 0; matrix products, arithmetic and copies ran while one was open for 0% -> 0% of each run, Pallas kernels for 0% -> 0%
where the time goes in v1:
time: 517 us; the launch traced here: 509 us
  Pallas kernels  217 us (42%)
  matrix products  187 us (36%)
  other arithmetic  83.7 us (16%)
  local copies, waits for them, and re-layouts  19.7 us (4%)
    pallas_call x1, Pallas kernels, group_sum(): pl.pallas_call(sum_kernel, out_shape=(jax.ShapeDtypeStruct((MATS * ROWS,...  217 us
    dot_general x5, matrix products, layer(): gate = jnp.dot(a, w['w_gate'], preferred_element_type=jnp.float32)  72.2 us
    dot_general x5, matrix products, layer(): up = jnp.dot(a, w['w_up'], preferred_element_type=jnp.float32)  64 us
    convert_element_type x2, other arithmetic, adamw(): return ((w - 0.02 * step).astype(jnp.bfloat16), m, v)  63.6 us
    dot_general x5, matrix products, matmul(): jnp.dot(a, w, preferred_element_type=jnp.float32).astype(jnp.bfloat16)  50.6 us
    mul x1, other arithmetic, clipped(): return [g * factor for g in gradients]  14.4 us
    mul x1, local copies, waits for them, and re-layouts, clipped(): return [g * factor for g in gradients]  12.1 us

profile of v1, /device:TPU:0, one launch (start us, length us, event | category | flops | bytes accessed | tf_op | source)
XLA Modules:
  0.0 509.5 jit_solution(17223440694979327136)
XLA Ops:
  0.6 3.2 copy.20
  4.6 12.9 %fusion.62 = f32[2048,1792]{1,0:T(8,128)} fusion(bf16[2,768,1792]{2,1,0:T(8,128)(2,1)} %param.13, bf16[1,2048,768]{2,1,0:T(8,128)(2,1)} %param.11, f32[2048]{0:T(1024)S(1)} %add_rsqrt_fusion), kind=kOutput, calls=%fused_computation.95 | convolution fusion | flops 5641863168 | bytes 20586496 | tf_op jit(solution)/shard_map/dot_general | solution.py:23
  17.5 16.2 %multiply_convert_fusion.1 = (bf16[2048,1792]{1,0:T(8,128)(2,1)}, f32[2048,1792]{1,0:T(8,128)}) fusion(f32[2048,1792]{1,0:T(8,128)} %fusion.62, bf16[2,768,1792]{2,1,0:T(8,128)(2,1)S(1)} %bitcast.81, bf16[1,2048,768]{2,1,0:T(8,128)(2,1)} %param.11, f32[2048]{0:T(1024)S(1)} %add_rsqrt_fusion), kind=kOutput, calls=%fused_computation.20 | convolution fusion | flops 5663883264 | bytes 42606592 | tf_op jit(solution)/shard_map/dot_general | solution.py:24
  33.7 9.5 %fusion.32 = (f32[2048]{0:T(1024)S(1)}, bf16[2048,768]{0,1:T(8,128)(2,1)S(1)}) fusion(bf16[2048,1792]{1,0:T(8,128)(2,1)} %get-tuple-element.25, bf16[2,1792,768]{2,1,0:T(8,128)(2,1)} %param.15, bf16[1,2048,768]{1,2,0:T(8,128)(2,1)S(1)} %copy.20), kind=kOutput, calls=%fused_computation.65 | convolution fusion | flops 5645006848 | bytes 16392192 | tf_op jit(solution)/shard_map/dot_general | solution.py:12
  43.3 9.5 %fusion.51 = f32[2048,1792]{1,0:T(8,128)} fusion(bf16[2,768,1792]{2,1,0:T(8,128)(2,1)S(1)} %bitcast.81, bf16[2048,768]{0,1:T(8,128)(2,1)S(1)} %get-tuple-element.28, f32[2048]{0:T(1024)S(1)} %fusion.85), kind=kOutput, calls=%fused_computation.84 | convolution fusion | flops 5641863168 | bytes 20586496 | tf_op jit(solution)/shard_map/jvp()/dot_general | solution.py:24
  52.8 8.0 %convolution_convert_fusion.1 = bf16[2048,1792]{1,0:T(8,128)(2,1)} fusion(bf16[1,2048,768]{2,1,0:T(8,128)(2,1)S(1)} %copy-done.2, bf16[2,1792,768]{2,1,0:T(8,128)(2,1)S(1)} %bitcast.83), kind=kOutput, calls=%fused_computation.58 | convolution fusion | flops 5640814592 | bytes 13238272 | tf_op jit(solution)/shard_map/transpose(jvp())/dot_general | solution.py:12
  60.8 23.2 %fusion.2 = (bf16[2048,1792]{1,0:T(8,128)(2,1)}, f32[2048,1792]{1,0:T(8,128)}) fusion(f32[2048,1792]{1,0:T(8,128)} %fusion.51, bf16[2048,1792]{1,0:T(8,128)(2,1)} %convolution_convert_fusion.1, bf16[2,768,1792]{2,1,0:T(8,128)(2,1)} %param.13, bf16[2048,768]{0,1:T(8,128)(2,1)} %copy-done.3, f32[2048]{0:T(1024)S(1)} %fusion.85), kind=kOutput, calls=%fused_computation.11 | convolution fusion | flops 5685903360 | bytes 49946624 | tf_op jit(solution)/shard_map/jvp()/dot_general | solution.py:23
  84.0 14.4 %fusion.46.refs_5_ = bf16[768,1792]{1,0:T(8,128)(2,1)} fusion(f32[2048,1792]{1,0:T(8,128)} %fusion.51, bf16[1,2048,768]{2,1,0:T(8,128)(2,1)S(1)} %copy-done.2, f32[2048,1792]{1,0:T(8,128)} %get-tuple-element.30), kind=kOutput, calls=%fused_computation.83 | convolution fusion | flops 5660540928 | bytes 35258368 | tf_op jit(solution)/shard_map/transpose(jvp())/dot_general | solution.py:12
  98.4 9.1 %convolution_convert_fusion.4 = bf16[2048,768]{0,1:T(8,128)(2,1)S(1)} fusion(bf16[2048,1792]{1,0:T(8,128)(2,1)} %get-tuple-element.29, bf16[2,768,1792]{2,1,0:T(8,128)(2,1)} %param.13), kind=kOutput, calls=%fused_computation.71 | convolution fusion | flops 5637144576 | bytes 13238272 | tf_op jit(solution)/shard_map/transpose(jvp())/dot_general | solution.py:23
  107.6 13.0 %fusion.34 = (f32[2048]{0:T(1024)S(1)}, bf16[2048,768]{0,1:T(8,128)(2,1)}) fusion(bf16[2048,768]{0,1:T(8,128)(2,1)S(1)} %copy-done.4, bf16[2048,768]{0,1:T(8,128)(2,1)S(1)} %convolution_convert_fusion.4, bf16[2,768,1792]{2,1,0:T(8,128)(2,1)} %param.14, bf16[2048,1792]{1,0:T(8,128)(2,1)} %convolution_convert_fusion.1, f32[2048,1792]{1,0:T(8,128)} %get-tuple-element.30), kind=kOutput, calls=%fused_computation.67 | convolution fusion | flops 5668599808 | bytes 34217984 | tf_op jit(solution)/shard_map/transpose(jvp())/dot_general | solution.py:24
  120.6 3.2 copy.21
  123.8 5.0 fusion.43
  128.9 10.6 %convolution_convert_fusion.2.refs_4_ = bf16[768,1792]{1,0:T(8,128)(2,1)} fusion(bf16[2048,768]{0,1:T(8,128)(2,1)S(1)} %fusion.43, bf16[2048,1792]{1,0:T(8,128)(2,1)} %get-tuple-element.25), kind=kOutput, calls=%fused_computation.69 | convolution fusion | flops 5638520832 | bytes 13238272 | tf_op jit(solution)/shard_map/transpose(jvp())/dot_general | solution.py:12
  139.5 12.6 %fusion.37.refs_3_ = bf16[768,1792]{1,0:T(8,128)(2,1)} fusion(bf16[2048,1792]{1,0:T(8,128)(2,1)} %convolution_convert_fusion.1, bf16[2048,768]{0,1:T(8,128)(2,1)S(1)} %copy-done.5, f32[2048]{0:T(1024)S(1)} %fusion.85, f32[2048,1792]{1,0:T(8,128)} %get-tuple-element.30), kind=kOutput, calls=%fused_computation.75 | convolution fusion | flops 5665259520 | bytes 27926528 | tf_op jit(solution)/shard_map/transpose(jvp())/dot_general | solution.py:24
  152.1 8.1 %convolution_convert_fusion = bf16[2048,1792]{1,0:T(8,128)(2,1)} fusion(bf16[2048,768]{0,1:T(8,128)(2,1)S(1)} %fusion.43, bf16[2,1792,768]{2,1,0:T(8,128)(2,1)S(1)} %bitcast.85), kind=kOutput, calls=%fused_computation.57 | convolution fusion | flops 5640814592 | bytes 13238272 | tf_op jit(solution)/shard_map/transpose(jvp())/dot_general | solution.py:12
  160.2 12.7 %fusion.41.refs_2_ = bf16[768,1792]{1,0:T(8,128)(2,1)} fusion(bf16[2048,1792]{1,0:T(8,128)(2,1)} %convolution_convert_fusion, bf16[1,2048,768]{1,2,0:T(8,128)(2,1)S(1)} %copy-done.1, f32[2048]{0:T(1024)S(1)} %copy-done.9, f32[2048,1792]{1,0:T(8,128)} %fusion.62), kind=kOutput, calls=%fused_computation.77 | convolution fusion | flops 5665259520 | bytes 27926528 | tf_op jit(solution)/shard_map/transpose(jvp())/dot_general | solution.py:24
  172.9 10.2 %convolution_convert_fusion.3.refs_1_ = bf16[768,1792]{1,0:T(8,128)(2,1)} fusion(bf16[2048,1792]{1,0:T(8,128)(2,1)} %get-tuple-element.29, bf16[2048,768]{0,1:T(8,128)(2,1)S(1)} %copy-done.5, f32[2048]{0:T(1024)S(1)} %fusion.85), kind=kOutput, calls=%fused_computation.70 | convolution fusion | flops 5641863168 | bytes 13246464 | tf_op jit(solution)/shard_map/transpose(jvp())/dot_general | solution.py:23
  183.1 16.7 %fusion.38.refs_0_ = bf16[768,1792]{1,0:T(8,128)(2,1)} fusion(f32[2048,1792]{1,0:T(8,128)} %fusion.62, f32[2048,1792]{1,0:T(8,128)} %get-tuple-element.26, bf16[2048,1792]{1,0:T(8,128)(2,1)} %convolution_convert_fusion, bf16[1,2048,768]{1,2,0:T(8,128)(2,1)S(1)} %copy-done.1, f32[2048]{0:T(1024)S(1)} %copy-done.9), kind=kOutput, calls=%fused_computation.76 | convolution fusion | flops 5683609600 | bytes 42606592 | tf_op jit(solution)/shard_map/transpose(jvp())/dot_general | solution.py:23
  199.8 217.2 %group_sum.1 = (bf16[4608,1792]{1,0:T(8,128)(2,1)}, f32[8,128]{1,0:T(8,128)}) custom-call(bf16[768,1792]{1,0:T(8,128)(2,1)} %fusion.38.refs_0_, bf16[768,1792]{1,0:T(8,128)(2,1)} %convolution_convert_fusion.3.refs_1_, bf16[768,1792]{1,0:T(8,128)(2,1)} %fusion.41.refs_2_, bf16[768,1792]{1,0:T(8,128)(2,1)} %fusion.37.refs_3_, ...), custom_call_target="tpu_custom_call" | custom-call | tf_op jit(solution)/shard_map/group_sum/pallas_call | solution.py:244
  417.1 1.2 slice.43
  419.0 14.4 %convert_multiply_fusion.9 = (f32[1536,1792]{1,0:T(8,128)}, f32[1536,1792]{1,0:T(8,128)S(1)}, f32[1536,1792]{1,0:T(8,128)}) fusion(bf16[4608,1792]{1,0:T(8,128)(2,1)} %get-tuple-element.11, f32[]{:T(128)} %bitcast.10), kind=kLoop, calls=%fused_computation.43 | loop fusion | flops 16515072 | bytes 49545220 | tf_op jit(solution)/shard_map/mul | solution.py:37
  433.3 40.4 %fusion.13 = (bf16[2,768,1792]{2,1,0:T(8,128)(2,1)}, f32[2,768,1792]{2,1,0:T(8,128)}, f32[2,768,1792]{2,1,0:T(8,128)}, bf16[2,768,1792]{2,1,0:T(8,128)(2,1)}, f3...) fusion(bf16[2,768,1792]{2,1,0:T(8,128)(2,1)} %param.13, f32[2,768,1792]{2,1,0:T(8,128)} %bitcast.79, ...), kind=kLoop, calls=%fused_computation.31 | loop fusion | flops 82575360 | bytes 132120576 | tf_op jit(solution)/shard_map/convert_element_type | solution.py:32
  473.7 12.1 %copy.23 = f32[2,768,1792]{1,2,0:T(8,128)} copy(f32[2,768,1792]{2,1,0:T(8,128)} %bitcast.77) | data formatting | bytes 22020096 | tf_op jit(solution)/shard_map/mul | solution.py:37
  485.8 23.3 %fusion.19 = (bf16[2,1792,768]{2,1,0:T(8,128)(2,1)}, f32[2,1792,768]{2,1,0:T(8,128)}, f32[2,1792,768]{2,1,0:T(8,128)}) fusion(bf16[2,1792,768]{2,1,0:T(8,128)(2,1)} %param.15, f32[2,768,1792]{1,2,0:T(8,128)} %copy.23, f32[2,1792,768]{2,1,0:T(8,128)} %param.21, f32[2,1792,768]{2,1,0:T(8,128)} %param.18), kind=kLoop, calls=%fused_computation.37 | loop fusion | flops 41287680 | bytes 66060288 | tf_op jit(solution)/shard_map/convert_element_type | solution.py:32
  (39 shorter events, 0.8 us)
Async XLA Ops:
  3.8 29.9 %copy-start = (bf16[1,2048,768]{1,2,0:T(8,128)(2,1)}, bf16[1,2048,768]{1,2,0:T(8,128)(2,1)S(1)}, u32[]{:S(2)}) copy-start(bf16[1,2048,768]{1,2,0:T(8,128)(2,1)S(1)} %copy.20) | copy-start | bytes 9437188
  3.9 13.6 %slice-start = ((s8[5505024]{0:T(1024)(128)(4,1)}), s8[4194304]{0:T(1024)(128)(4,1)S(1)}, s32[]{:S(2)}) async-start(s8[5505024]{0:T(1024)(128)(4,1)} %bitcast.80), calls=%async_computation | async-start | bytes 8388608
  4.5 12.9 %copy-start.8 = (f32[2048]{0:T(1024)}, f32[2048]{0:T(1024)S(1)}, u32[]{:S(2)}) copy-start(f32[2048]{0:T(1024)S(1)} %add_rsqrt_fusion) | copy-start | bytes 24580
  4.5 12.9 %slice-start.1 = ((s8[5505024]{0:T(1024)(128)(4,1)}), s8[1310720]{0:T(1024)(128)(4,1)S(1)}, s32[]{:S(2)}) async-start(s8[5505024]{0:T(1024)(128)(4,1)} %bitcast.80), calls=%async_computation.1 | async-start | bytes 2621440
  33.7 19.1 %slice-start.2 = ((s8[5505024]{0:T(1024)(128)(4,1)}), s8[1310720]{0:T(1024)(128)(4,1)S(1)}, s32[]{:S(2)}) async-start(s8[5505024]{0:T(1024)(128)(4,1)} %bitcast.82), calls=%async_computation.2 | async-start | bytes 2621440
  43.2 9.5 %copy-start.3 = (bf16[2048,768]{0,1:T(8,128)(2,1)}, bf16[2048,768]{0,1:T(8,128)(2,1)S(1)}, u32[]{:S(2)}) copy-start(bf16[2048,768]{0,1:T(8,128)(2,1)S(1)} %get-tuple-element.28) | copy-start | bytes 9437188
  43.3 9.5 %copy-start.6 = (f32[2048]{0:T(1024)}, f32[2048]{0:T(1024)S(1)}, u32[]{:S(2)}) copy-start(f32[2048]{0:T(1024)S(1)} %get-tuple-element.27) | copy-start | bytes 24580
  43.3 9.5 %slice-start.3 = ((s8[5505024]{0:T(1024)(128)(4,1)}), s8[4194304]{0:T(1024)(128)(4,1)S(1)}, s32[]{:S(2)}) async-start(s8[5505024]{0:T(1024)(128)(4,1)} %bitcast.82), calls=%async_computation.3 | async-start | bytes 8388608
  43.3 9.5 %copy-start.2 = (bf16[1,2048,768]{2,1,0:T(8,128)(2,1)S(1)}, bf16[1,2048,768]{2,1,0:T(8,128)(2,1)}, u32[]{:S(2)}) copy-start(bf16[1,2048,768]{2,1,0:T(8,128)(2,1)} %param.12) | copy-start | bytes 9437188
  98.4 9.1 %copy-start.4 = (bf16[2048,768]{0,1:T(8,128)(2,1)S(1)}, bf16[2048,768]{0,1:T(8,128)(2,1)}, u32[]{:S(2)}) copy-start(bf16[2048,768]{0,1:T(8,128)(2,1)} %copy-done.3) | copy-start | bytes 9437188
  107.6 13.1 %copy-start.7 = (f32[2048]{0:T(1024)S(1)}, f32[2048]{0:T(1024)}, u32[]{:S(2)}) copy-start(f32[2048]{0:T(1024)} %copy-done.6) | copy-start | bytes 24580
  128.9 10.6 %copy-start.5 = (bf16[2048,768]{0,1:T(8,128)(2,1)S(1)}, bf16[2048,768]{0,1:T(8,128)(2,1)}, u32[]{:S(2)}) copy-start(bf16[2048,768]{0,1:T(8,128)(2,1)} %copy-done.3) | copy-start | bytes 9437188
  128.9 23.2 %slice-start.4 = ((s8[5505024]{0:T(1024)(128)(4,1)}), s8[4194304]{0:T(1024)(128)(4,1)S(1)}, s32[]{:S(2)}) async-start(s8[5505024]{0:T(1024)(128)(4,1)} %bitcast.84), calls=%async_computation.4 | async-start | bytes 8388608
  139.5 12.6 %slice-start.5 = ((s8[5505024]{0:T(1024)(128)(4,1)}), s8[1310720]{0:T(1024)(128)(4,1)S(1)}, s32[]{:S(2)}) async-start(s8[5505024]{0:T(1024)(128)(4,1)} %bitcast.84), calls=%async_computation.5 | async-start | bytes 2621440
  152.1 8.1 %copy-start.1 = (bf16[1,2048,768]{1,2,0:T(8,128)(2,1)S(1)}, bf16[1,2048,768]{1,2,0:T(8,128)(2,1)}, u32[]{:S(2)}) copy-start(bf16[1,2048,768]{1,2,0:T(8,128)(2,1)} %copy-done) | copy-start | bytes 9437188
  152.1 8.1 %copy-start.9 = (f32[2048]{0:T(1024)S(1)}, f32[2048]{0:T(1024)}, u32[]{:S(2)}) copy-start(f32[2048]{0:T(1024)} %copy-done.8) | copy-start | bytes 24580

commit v2 on v1

v2 whole, which is shorter than its diff:
```python
import functools

import jax
import jax.numpy as jnp
from jax import lax
from jax.experimental import pallas as pl
from jax.experimental.pallas import tpu as pltpu
from jax.sharding import PartitionSpec as P

BF, F32 = jnp.bfloat16, jnp.float32


def dot(a, b):
    return jnp.dot(a, b, preferred_element_type=F32)


def dot_t(a, b):
    return lax.dot_general(a, b, (((1,), (1,)), ((), ())), preferred_element_type=F32)


def normed(h):
    wide = h.astype(F32)
    scale = lax.rsqrt(jnp.mean(wide**2, -1, keepdims=True) + 1e-6)
    return (wide * scale).astype(BF)


def sigmoid(x):
    return 1.0 / (1.0 + jnp.exp(-x))


def by_gate_and_up(gate, up, by_p):
    s = sigmoid(gate)
    silu = gate * s
    by_p = by_p.astype(BF).astype(F32)
    return (by_p * up * (s + silu * (1.0 - s))).astype(BF), (by_p * silu).astype(BF), (silu * up).astype(BF)


TOKENS, ROWS, COLS = 2048, 768, 1792
BLOCK = 512
TILE = 256
TILES = COLS // TILE


def forward_kernel(x, dy, w_gate, w_up, w_down, a0_out, p0_out, h1_out, a1_out, p1_out, bg_out, bu_out, *scratch):
    weights, sem = scratch[:6], scratch[6]
    copies = [pltpu.make_async_copy(w.at[n], weights[3 * n + i], sem.at[3 * n + i]) for n in range(2) for i, w in enumerate((w_gate, w_up, w_down))]

    first = pl.program_id(0) == 0

    @pl.when(first)
    def _():
        for copy in copies:
            copy.start()

    a0 = normed(x[...])
    a0_out[...] = a0

    def ready(*which):
        @pl.when(first)
        def _():
            for i in which:
                copies[i].wait()

    ready(0, 1)
    for n in range(TILES):
        at = slice(n * TILE, (n + 1) * TILE)
        gate, up = dot(a0_out[...], weights[0][:, at]), dot(a0_out[...], weights[1][:, at])
        p0_out[:, at] = (gate * sigmoid(gate) * up).astype(BF)
    ready(2)
    h1_out[...] = x[...] + dot(p0_out[...], weights[2][...]).astype(BF)
    a1_out[...] = normed(h1_out[...])
    ready(3, 4, 5)
    for n in range(TILES):
        at = slice(n * TILE, (n + 1) * TILE)
        gate, up = dot(a1_out[...], weights[3][:, at]), dot(a1_out[...], weights[4][:, at])
        bg_out[:, at], bu_out[:, at], p1_out[:, at] = by_gate_and_up(gate, up, dot_t(dy[...], weights[5][at, :]))


def forward(x, dy, w_gate, w_up, w_down):
    narrow, wide = pl.BlockSpec((BLOCK, ROWS), lambda i: (i, 0)), pl.BlockSpec((BLOCK, COLS), lambda i: (i, 0))
    of = lambda n: jax.ShapeDtypeStruct((TOKENS, n), BF)
    return pl.pallas_call(
        forward_kernel,
        grid=(TOKENS // BLOCK,),
        out_shape=(of(ROWS), of(COLS), of(ROWS), of(ROWS), of(COLS), of(COLS), of(COLS)),
        in_specs=[narrow, narrow] + [pl.BlockSpec(memory_space=pl.ANY)] * 3,
        out_specs=(narrow, wide, narrow, narrow, wide, wide, wide),
        scratch_shapes=[pltpu.VMEM(s, BF) for _ in range(2) for s in ((ROWS, COLS), (ROWS, COLS), (COLS, ROWS))] + [pltpu.SemaphoreType.DMA((6,))],
        compiler_params=pltpu.CompilerParams(vmem_limit_bytes=60 * 2**20),
        name="forward",
    )(x, dy, w_gate, w_up, w_down)


def adamw_kernel(transposed, squares, g, w, m, v, w_out, m_out, v_out):
    count = 2 * 3 * ROWS * COLS
    factor = jnp.minimum(1.0, 0.5 * lax.rsqrt(squares[...] / count + 1e-30))[0:1, 0:1]
    g = (g[...].T if transposed else g[...]).astype(F32) * factor
    m = 0.9 * m[0] + 0.1 * g
    v = 0.95 * v[0] + 0.05 * g * g
    w = w[0].astype(F32)
    w_out[0] = (w - 0.02 * (m * lax.rsqrt(v + 1e-8) + 0.1 * w)).astype(BF)
    m_out[0] = m
    v_out[0] = v


def adamw(kind, squares, summed, w, m, v):
    transposed = w.shape[1] == COLS
    layers = w.shape[0]
    block = 256
    if transposed:
        steps = COLS // block
        own, grad = pl.BlockSpec((1, block, ROWS), lambda n, i: (n, i, 0)), pl.BlockSpec((ROWS, block), lambda n, i: (kind * layers + n, i))
    else:
        steps = ROWS // block
        own, grad = pl.BlockSpec((1, block, COLS), lambda n, i: (n, i, 0)), pl.BlockSpec((block, COLS), lambda n, i: ((kind * layers + n) * steps + i, 0))
    return pl.pallas_call(
        functools.partial(adamw_kernel, transposed),
        grid=(layers, steps),
        out_shape=(jax.ShapeDtypeStruct(w.shape, BF), jax.ShapeDtypeStruct(w.shape, F32), jax.ShapeDtypeStruct(w.shape, F32)),
        in_specs=[pl.BlockSpec((8, 128), lambda n, i: (0, 0)), grad, own, own, own],
        out_specs=(own, own, own),
        compiler_params=pltpu.CompilerParams(vmem_limit_bytes=60 * 2**20),
        name="adamw",
    )(squares, summed, w, m, v)


MESH = pl.DeviceIdType.MESH
MATS = 6
HALF, QUARTER = ROWS // 2, ROWS // 4
SUB = 4
PIECE = QUARTER // SUB
N = MATS * SUB
SKEW = 2
LINE = 4


def place(q):
    return lax.rem(lax.rem(q, 3) + 2, 3) * 2 + 1 - q // 3


SLOTS = 4


def backward_kernel(*refs):
    dy_in, a0_in, p0_in, h1_in, a1_in, p1_in, bg_in, bu_in, wg_in, wu_in, wd_in = refs[:11]
    out, squares_out, t, p, r, bg, bu, lhs, by_h, small, wg, wu, wd, acc, tile, sq = refs[11:27]
    load, xs, xr, right_s, left_s, rs_r, ag_r, d_s, d_r, out_s, sq_s, sq_r = refs[27:]
    dp = lax.axis_index("dp")
    z, c = dp // 2, lax.rem(dp, 2)
    other = z * 2 + 1 - c

    def fetch(src, dst, n):
        return pltpu.make_async_copy(src, dst, load.at[n])

    get_dy, get_p1, get_bg = fetch(dy_in, by_h, 0), fetch(p1_in, bu, 1), fetch(bg_in, bg, 2)
    get_a1, get_wg1, get_wu1, get_wd0 = fetch(a1_in, small, 3), fetch(wg_in.at[1], wg, 4), fetch(wu_in.at[1], wu, 5), fetch(wd_in.at[0], wd, 6)
    get_bu, get_h1 = fetch(bu_in, bu, 7), fetch(h1_in, small, 8)
    get_p0, get_a0, get_wg0, get_wu0 = fetch(p0_in, bu, 9), fetch(a0_in, small, 10), fetch(wg_in.at[0], wg, 11), fetch(wu_in.at[0], wu, 12)
    for copy in (get_dy, get_p1, get_bg, get_a1, get_wg1, get_wu1, get_wd0):
        copy.start()
    barrier = pltpu.get_barrier_semaphore()
    for step in range(1, 8):
        pl.semaphore_signal(barrier, inc=1, device_id={"dp": lax.rem(dp + step, 8)}, device_id_type=MESH)
    pl.semaphore_wait(barrier, 7)
    acc[...] = jnp.zeros_like(acc)

    def own(q, row, rows):
        return pl.ds(pl.multiple_of(lax.rem(q, SLOTS) * ROWS + row, 16), rows)

    def exchange(q, x):
        return pltpu.make_async_remote_copy(
            src_ref=t.at[own(q, (1 - c) * HALF + x * QUARTER, QUARTER)],
            dst_ref=p.at[pl.ds(pl.multiple_of(place(q) * HALF + x * QUARTER, 16), QUARTER)],
            send_sem=xs.at[x * MATS + q],
            recv_sem=xr.at[x * MATS + q],
            device_id={"dp": other},
            device_id_type=MESH,
        )

    def turned(src):
        @pl.loop(0, TOKENS // TILE)
        def _(i):
            at = pl.ds(pl.multiple_of(i * TILE, TILE), TILE)
            lhs[:, at] = src[at, :].T

    def gradient(q, right, lo, hi):
        @pl.loop(lo, hi)
        def _(n):
            at = pl.ds(pl.multiple_of(n * TILE, TILE), TILE)
            t[own(q, 0, ROWS), at] = dot(lhs[...], right[:, at]).astype(BF)

    def send_terms(q):
        for x in range(2):
            exchange(q, x).start()

    get_dy.wait()
    turned(by_h)
    get_p1.wait()
    gradient(0, bu, 0, TILES)
    send_terms(0)
    get_bu.start()

    def through_layer(i):
        at = pl.ds(pl.multiple_of(i * BLOCK, BLOCK), BLOCK)
        by_a = dot_t(bg[at, :], wg[...]).astype(BF) + dot_t(bu[at, :], wu[...]).astype(BF)
        by_a, wide_h = by_a.astype(F32), small[at, :].astype(F32)
        scale = lax.rsqrt(jnp.mean(wide_h * wide_h, -1, keepdims=True) + 1e-6)
        inner = jnp.mean(by_a * wide_h, -1, keepdims=True)
        by_h[at, :] = by_h[at, :] + (by_a * scale - wide_h * (scale * scale * scale * inner)).astype(BF)

    def first_layer(i):
        rows = pl.ds(pl.multiple_of(i // TILES * BLOCK, BLOCK), BLOCK)
        at = pl.ds(pl.multiple_of(lax.rem(i, TILES) * TILE, TILE), TILE)
        gate, up = dot(small[rows, :], wg[:, at]), dot(small[rows, :], wu[:, at])
        bg[rows, at], bu[rows, at], _ = by_gate_and_up(gate, up, dot_t(by_h[rows, :], wd[at, :]))

    def work(i):
        @pl.when(i == 0)
        def _():
            get_a1.wait()
            turned(small)
            get_h1.start()
            get_bg.wait()

        @pl.when(i < 3)
        def _():
            gradient(1, bg, lax.select(i == 0, 0, 3 * i - 1), jnp.minimum(3 * i + 2, TILES))

        @pl.when(i == 2)
        def _():
            send_terms(1)

        @pl.when(i == 3)
        def _():
            get_bu.wait()

        @pl.when(jnp.logical_and(i >= 3, i < 6))
        def _():
            gradient(2, bu, 3 * (i - 3), jnp.minimum(3 * (i - 2), TILES))

        @pl.when(i == 5)
        def _():
            send_terms(2)

        @pl.when(i == 4)
        def _():
            for copy in (get_wg1, get_wu1, get_h1):
                copy.wait()

        @pl.when(jnp.logical_and(i >= 4, i < 8))
        def _():
            through_layer(i - 4)

        @pl.when(i == 7)
        def _():
            for copy in (get_p0, get_a0, get_wg0, get_wu0):
                copy.start()

        @pl.when(i == 8)
        def _():
            turned(by_h)
            get_p0.wait()

        @pl.when(jnp.logical_and(i >= 8, i < 11))
        def _():
            gradient(3, bu, lax.select(i == 8, 0, 3 * (i - 8) - 1), jnp.minimum(3 * (i - 8) + 2, TILES))

        @pl.when(i == 10)
        def _():
            send_terms(3)

        @pl.when(i == 11)
        def _():
            for copy in (get_a0, get_wg0, get_wu0, get_wd0):
                copy.wait()
            turned(small)

        @pl.when(jnp.logical_and(i >= 11, i < 15))
        def _():
            pl.loop(0, TILES)(lambda n: first_layer((i - 11) * TILES + n))

        @pl.when(i == 15)
        def _():
            for x in range(2):
                exchange(0, x).wait_send()
            gradient(4, bg, 0, TILES)
            send_terms(4)

        @pl.when(i == 16)
        def _():
            for x in range(2):
                exchange(1, x).wait_send()

        @pl.when(jnp.logical_and(i >= 16, i < 19))
        def _():
            gradient(5, bu, 3 * (i - 16), jnp.minimum(3 * (i - 15), TILES))

        @pl.when(i == 18)
        def _():
            send_terms(5)

    def wide(k, x, core):
        m = place(k // SUB)
        return pl.ds(pl.multiple_of(m * ROWS + core * HALF + x * QUARTER + lax.rem(k, SUB) * PIECE, 16), PIECE)

    def term(k, x):
        return own(k // SUB, c * HALF + x * QUARTER + lax.rem(k, SUB) * PIECE, PIECE)

    def narrow(k, x):
        m = place(k // SUB)
        return pl.ds(pl.multiple_of(m * HALF + x * QUARTER + lax.rem(k, SUB) * PIECE, 16), PIECE)

    def sum_copy(k, x):
        return pltpu.make_async_remote_copy(
            src_ref=p.at[narrow(k, x)],
            dst_ref=r.at[narrow(k, x)],
            send_sem=right_s if x == 0 else left_s,
            recv_sem=rs_r.at[x * N + k],
            device_id={"dp": dp + 2 if x == 0 else dp - 2},
            device_id_type=MESH,
        )

    def back_copy(k, x, first=False):
        return pltpu.make_async_remote_copy(
            src_ref=r.at[narrow(k, x)] if first else out.at[wide(k, x, c)],
            dst_ref=out.at[wide(k, x, c)],
            send_sem=left_s if x == 0 else right_s,
            recv_sem=ag_r.at[x * N + k],
            device_id={"dp": dp - 2 if x == 0 else dp + 2},
            device_id_type=MESH,
        )

    def share_copy(k, x, first=False):
        return pltpu.make_async_remote_copy(
            src_ref=r.at[narrow(k, x)] if first else out.at[wide(k, x, c)],
            dst_ref=out.at[wide(k, x, c)],
            send_sem=d_s,
            recv_sem=d_r.at[x * N + k],
            device_id={"dp": other},
            device_id_type=MESH,
        )

    def share_arrival(k, x):
        return pltpu.make_async_remote_copy(
            src_ref=out.at[wide(k, x, 1 - c)],
            dst_ref=out.at[wide(k, x, 1 - c)],
            send_sem=d_s,
            recv_sem=d_r.at[x * N + k],
            device_id={"dp": other},
            device_id_type=MESH,
        )

    def valid(k):
        return jnp.logical_and(k >= 0, k < N)

    def add(k, x):
        hops = z if x == 0 else LINE - 1 - z

        @pl.when(lax.rem(k, SUB) == 0)
        def _():
            exchange(k // SUB, x).wait_recv()

        mine = t[term(k, x), :].astype(jnp.float32) + p[narrow(k, x), :].astype(jnp.float32)

        @pl.when(hops == 0)
        def _():
            p[narrow(k, x), :] = mine.astype(jnp.bfloat16)
            sum_copy(k, x).start()

        @pl.when(hops > 0)
        def _():
            sum_copy(k, x).wait_recv()
            mine = t[term(k, x), :].astype(jnp.float32) + p[narrow(k, x), :].astype(jnp.float32)
            total = (mine + r[narrow(k, x), :].astype(jnp.float32)).astype(jnp.bfloat16)

            @pl.when(hops < LINE - 1)
            def _():
                p[narrow(k, x), :] = total
                sum_copy(k, x).start()

            @pl.when(hops == LINE - 1)
            def _():
                r[narrow(k, x), :] = total
                back_copy(k, x, True).start()
                share_copy(k, x, True).start()
                pltpu.make_async_copy(r.at[narrow(k, x)], out.at[wide(k, x, c)], out_s).start()
                g = total.astype(jnp.float32)
                acc[...] += jnp.sum((g * g).reshape(PIECE // 8, 8, COLS), axis=0)

    def relay(k, x):
        back_copy(k, x).wait_recv()

        @pl.when((z if x == 0 else LINE - 1 - z) > 0)
        def _():
            back_copy(k, x).start()

        share_copy(k, x).start()

    turn = SKEW * (LINE - 1)

    @pl.loop(0, N + 2 * turn + 1)
    def _(i):
        for x in range(2):
            k = i - SKEW * (z if x == 0 else LINE - 1 - z)
            pl.when(valid(k))(lambda k=k, x=x: add(k, x))
        for x in range(2):
            back = LINE - 1 - z if x == 0 else z
            k = i - turn - SKEW * back
            pl.when(jnp.logical_and(back > 0, valid(k)))(lambda k=k, x=x: relay(k, x))
            k = k - 1

            @pl.when(valid(k))
            def _(k=k, x=x):
                share_arrival(k, x).wait_recv()

        work(i)

    total = jnp.sum(acc[...])
    tile[...] = jnp.full(tile.shape, total, jnp.float32)

    def tell(slot, step):
        return pltpu.make_async_remote_copy(
            src_ref=tile, dst_ref=sq.at[slot], send_sem=sq_s.at[step - 1], recv_sem=sq_r.at[slot],
            device_id={"dp": lax.rem(dp + step, 8)}, device_id_type=MESH,
        )

    for slot, owner in enumerate((0, 1, 6, 7)):
        @pl.when(dp == owner)
        def _(slot=slot):
            for step in range(1, 8):
                tell(slot, step).start()
            sq[slot] = tile[...]

        @pl.when(dp != owner)
        def _(slot=slot):
            tell(slot, 1).wait_recv()

    squares_out[...] = sq[0] + sq[1] + sq[2] + sq[3]

    for slot, owner in enumerate((0, 1, 6, 7)):
        @pl.when(dp == owner)
        def _(slot=slot):
            for step in range(1, 8):
                tell(slot, step).wait_send()

    def all_sent(sem):
        pltpu.make_async_remote_copy(
            src_ref=p, dst_ref=p, send_sem=sem, recv_sem=xr.at[0], device_id={"dp": other}, device_id_type=MESH
        ).wait_send()

    pl.when(z < LINE - 1)(lambda: all_sent(right_s))
    pl.when(z > 0)(lambda: all_sent(left_s))
    all_sent(d_s)
    for q in range(2, MATS):
        for x in range(2):
            exchange(q, x).wait_send()

    @pl.when(jnp.logical_or(z == 0, z == LINE - 1))
    def _():
        pltpu.make_async_copy(r.at[pl.ds(0, N * PIECE)], out.at[pl.ds(0, N * PIECE)], out_s).wait()


def backward(arrays):
    dma = pltpu.SemaphoreType.DMA
    vmem = pltpu.VMEM
    return pl.pallas_call(
        backward_kernel,
        out_shape=(jax.ShapeDtypeStruct((MATS * ROWS, COLS), BF), jax.ShapeDtypeStruct((8, 128), F32)),
        in_specs=[pl.BlockSpec(memory_space=pl.ANY)] * len(arrays),
        out_specs=(pl.BlockSpec(memory_space=pl.ANY), pl.BlockSpec(memory_space=pltpu.VMEM)),
        scratch_shapes=[
            vmem((SLOTS * ROWS, COLS), BF),
            vmem((MATS * HALF, COLS), BF),
            vmem((MATS * HALF, COLS), BF),
            vmem((TOKENS, COLS), BF),
            vmem((TOKENS, COLS), BF),
            vmem((ROWS, TOKENS), BF),
            vmem((TOKENS, ROWS), BF),
            vmem((TOKENS, ROWS), BF),
            vmem((ROWS, COLS), BF),
            vmem((ROWS, COLS), BF),
            vmem((COLS, ROWS), BF),
            vmem((8, COLS), F32),
            vmem((8, 128), F32),
            vmem((4, 8, 128), F32),
            dma((13,)), dma((2 * MATS,)), dma((2 * MATS,)), dma(()), dma(()), dma((2 * N,)), dma((2 * N,)), dma(()), dma((2 * N,)), dma(()),
            dma((7,)), dma((4,)),
        ],
        compiler_params=pltpu.CompilerParams(collective_id=0, has_side_effects=True, vmem_limit_bytes=67043328),
        name="backward",
    )(*arrays)


def solution(mesh):
    def step(x, dy, *arrays):
        weights, m, v = (arrays[i : i + 3] for i in (0, 3, 6))
        x, dy = x[0], dy[0]
        kept = forward(x, dy, *weights)
        summed, squares = backward((dy, *kept, *weights))
        new = [adamw(i, squares, summed, *one) for i, one in enumerate(zip(weights, m, v, strict=True))]
        return tuple(one[which] for which in range(3) for one in new)

    return jax.shard_map(
        step,
        mesh=mesh,
        in_specs=(P(("rep", "dp"), None, None),) * 2 + (P(None, None, None),) * 9,
        out_specs=(P("rep", None, None),) * 9,
        check_vma=False,
    )
```

time: 517 us -> 351 us (0.68); the launches traced: 509 us -> 351 us
  matrix products: 187 us -> 0 us
  Pallas kernels: 217 us -> 350 us
  other arithmetic: 83.7 us -> 0 us
  local copies, waits for them, and re-layouts: 19.7 us -> 0 us
    dot_general x15 -> x0, matrix products: 187 us -> none  [the longest x5 72.2 us: layer(): gate = jnp.dot(a, w['w_gate'], preferred_element_type=jnp.float32)]
    pallas_call x1 -> x5, Pallas kernels: 217 us -> 350 us  [the longest x1 231 us: backward(): pl.pallas_call(backward_kernel, out_shape=(jax.ShapeDtypeStruct((MATS * R...]
    convert_element_type x2 -> x0, other arithmetic: 63.6 us -> none  [adamw(): return ((w - 0.02 * step).astype(jnp.bfloat16), m, v)]
    mul x2 -> x0, other arithmetic: 14.4 us -> none  [the longest x1 14.4 us: clipped(): return [g * factor for g in gradients]]
    mul x1 -> x0, local copies, waits for them, and re-layouts: 12.1 us -> none  [clipped(): return [g * factor for g in gradients]]
    unnamed x34 -> x0, local copies, waits for them, and re-layouts: 6.47 us -> none
where the time goes in v2:
time: 351 us
  Pallas kernels  350 us (100%)
    pallas_call x1, Pallas kernels, backward(): pl.pallas_call(backward_kernel, out_shape=(jax.ShapeDtypeStruct((MATS * R...  231 us
    pallas_call x3, Pallas kernels, adamw(): pl.pallas_call(functools.partial(adamw_kernel, transposed), grid=(layers,...  69.1 us
    pallas_call x1, Pallas kernels, forward(): pl.pallas_call(forward_kernel, grid=(TOKENS // BLOCK,), out_shape=(of(ROW...  50 us

profile of v2, /device:TPU:0, one launch (start us, length us, event | category | flops | bytes accessed | tf_op | source)
XLA Modules:
  0.0 350.5 jit_solution(2681045292566195288)
XLA Ops:
  0.6 50.0 %forward.1 = (bf16[2048,768]{1,0:T(8,128)(2,1)}, bf16[2048,1792]{1,0:T(8,128)(2,1)}, bf16[2048,768]{1,0:T(8,128)(2,1)}, bf16[2048,768]{1,0:T(8,128)(2,1)}, bf16[...) custom-call(bf16[2048,768]{1,0:T(8,128)(2,1)} %bitcast.4, ...), custom_call_target="tpu_custom_call" | custom-call | tf_op jit(solution)/shard_map/forward/pallas_call | solution.py:82
  50.6 230.8 %backward.1 = (bf16[4608,1792]{1,0:T(8,128)(2,1)}, f32[8,128]{1,0:T(8,128)}) custom-call(bf16[2048,768]{1,0:T(8,128)(2,1)} %bitcast.3, bf16[2048,768]{1,0:T(8,128)(2,1)} %get-tuple-element.27.refs_1_, bf16[2048,1792]{1,0:T(8,128)(2,1)} %get-tuple-element.28.refs_2_, bf16[2048,768]{1,0:T(8,128)(2,1)} %get-tuple-element.29.refs_3_, ...), custom_call_target="tpu_custom_call" | custom-call | tf_op jit(solution)/shard_map/backward/pallas_call | solution.py:466
  281.4 25.9 %adamw.5 = (bf16[2,1792,768]{2,1,0:T(8,128)(2,1)}, f32[2,1792,768]{2,1,0:T(8,128)}, f32[2,1792,768]{2,1,0:T(8,128)}) custom-call(f32[8,128]{1,0:T(8,128)} %get-tuple-element.34.squares, bf16[4608,1792]{1,0:T(8,128)(2,1)} %get-tuple-element.35.g, bf16[2,1792,768]{2,1,0:T(8,128)(2,1)} %w.5, f32[2,1792,768]{2,1,0:T(8,128)} %m.5, f32[2,1792,768]{2,1,0:T(8,128)} %v.5), custom_call_target="tpu_custom_call" | custom-call | tf_op jit(solution)/shard_map/adamw/pallas_call | solution.py:116
  307.3 21.6 %adamw.4 = (bf16[2,768,1792]{2,1,0:T(8,128)(2,1)}, f32[2,768,1792]{2,1,0:T(8,128)}, f32[2,768,1792]{2,1,0:T(8,128)}) custom-call(f32[8,128]{1,0:T(8,128)} %get-tuple-element.34.squares, bf16[4608,1792]{1,0:T(8,128)(2,1)} %get-tuple-element.35.g, bf16[2,768,1792]{2,1,0:T(8,128)(2,1)} %w.4, f32[2,768,1792]{2,1,0:T(8,128)} %m.4, f32[2,768,1792]{2,1,0:T(8,128)} %v.4), custom_call_target="tpu_custom_call" | custom-call | tf_op jit(solution)/shard_map/adamw/pallas_call | solution.py:116
  328.9 21.6 %adamw.3 = (bf16[2,768,1792]{2,1,0:T(8,128)(2,1)}, f32[2,768,1792]{2,1,0:T(8,128)}, f32[2,768,1792]{2,1,0:T(8,128)}) custom-call(f32[8,128]{1,0:T(8,128)} %get-tuple-element.34.squares, bf16[4608,1792]{1,0:T(8,128)(2,1)} %get-tuple-element.35.g, bf16[2,768,1792]{2,1,0:T(8,128)(2,1)} %w.3, f32[2,768,1792]{2,1,0:T(8,128)} %m.3, f32[2,768,1792]{2,1,0:T(8,128)} %v.3), custom_call_target="tpu_custom_call" | custom-call | tf_op jit(solution)/shard_map/adamw/pallas_call | solution.py:116

commit v3 on v2

v3 whole, which is shorter than its diff:
```python
import functools

import jax
import jax.numpy as jnp
from jax import lax
from jax.experimental import pallas as pl
from jax.experimental.pallas import tpu as pltpu
from jax.sharding import PartitionSpec as P

BF, F32 = jnp.bfloat16, jnp.float32


def dot(a, b):
    return jnp.dot(a, b, preferred_element_type=F32)


def dot_t(a, b):
    return lax.dot_general(a, b, (((1,), (1,)), ((), ())), preferred_element_type=F32)


def normed(h):
    wide = h.astype(F32)
    scale = lax.rsqrt(jnp.mean(wide**2, -1, keepdims=True) + 1e-6)
    return (wide * scale).astype(BF)


def sigmoid(x):
    return 1.0 / (1.0 + jnp.exp(-x))


def by_gate_and_up(gate, up, by_p):
    s = sigmoid(gate)
    silu = gate * s
    by_p = by_p.astype(BF).astype(F32)
    return (by_p * up * (s + silu * (1.0 - s))).astype(BF), (by_p * silu).astype(BF), (silu * up).astype(BF)


TOKENS, ROWS, COLS = 2048, 768, 1792
BLOCK = 512
TILE = 256
TILES = COLS // TILE


def forward_kernel(x, dy, w_gate, w_up, w_down, dyt_out, a0_out, a0t_out, p0_out, h1_out, a1t_out, p1_out, bg_out, bu_out, *scratch):
    weights, a1, sem = scratch[:6], scratch[6], scratch[7]
    copies = [pltpu.make_async_copy(w.at[n], weights[3 * n + i], sem.at[3 * n + i]) for n in range(2) for i, w in enumerate((w_gate, w_up, w_down))]

    first = pl.program_id(0) == 0

    @pl.when(first)
    def _():
        for copy in copies:
            copy.start()

    a0 = normed(x[...])
    a0_out[...] = a0
    a0t_out[...] = a0.T
    dyt_out[...] = dy[...].T

    def ready(*which):
        @pl.when(first)
        def _():
            for i in which:
                copies[i].wait()

    ready(0, 1)
    for n in range(TILES):
        at = slice(n * TILE, (n + 1) * TILE)
        gate, up = dot(a0_out[...], weights[0][:, at]), dot(a0_out[...], weights[1][:, at])
        p0_out[:, at] = (gate * sigmoid(gate) * up).astype(BF)
    ready(2)
    h1_out[...] = x[...] + dot(p0_out[...], weights[2][...]).astype(BF)
    a1[...] = normed(h1_out[...])
    a1t_out[...] = a1[...].T
    ready(3, 4, 5)
    for n in range(TILES):
        at = slice(n * TILE, (n + 1) * TILE)
        gate, up = dot(a1[...], weights[3][:, at]), dot(a1[...], weights[4][:, at])
        bg_out[:, at], bu_out[:, at], p1_out[:, at] = by_gate_and_up(gate, up, dot_t(dy[...], weights[5][at, :]))


def forward(x, dy, w_gate, w_up, w_down):
    narrow, wide = pl.BlockSpec((BLOCK, ROWS), lambda i: (i, 0)), pl.BlockSpec((BLOCK, COLS), lambda i: (i, 0))
    turned = pl.BlockSpec((ROWS, BLOCK), lambda i: (0, i))
    of = lambda n: jax.ShapeDtypeStruct((TOKENS, n), BF)
    of_turned = jax.ShapeDtypeStruct((ROWS, TOKENS), BF)
    return pl.pallas_call(
        forward_kernel,
        grid=(TOKENS // BLOCK,),
        out_shape=(of_turned, of(ROWS), of_turned, of(COLS), of(ROWS), of_turned, of(COLS), of(COLS), of(COLS)),
        in_specs=[narrow, narrow] + [pl.BlockSpec(memory_space=pl.ANY)] * 3,
        out_specs=(turned, narrow, turned, wide, narrow, turned, wide, wide, wide),
        scratch_shapes=[pltpu.VMEM(s, BF) for _ in range(2) for s in ((ROWS, COLS), (ROWS, COLS), (COLS, ROWS))] + [pltpu.VMEM((BLOCK, ROWS), BF), pltpu.SemaphoreType.DMA((6,))],
        compiler_params=pltpu.CompilerParams(vmem_limit_bytes=60 * 2**20),
        name="forward",
    )(x, dy, w_gate, w_up, w_down)


DEPTH = 4
CUTS = (128, 256)
BLOCKS = (2 * ROWS // CUTS[0], 2 * COLS // CUTS[1])


def adamw_kernel(squares, g_in, *refs):
    arrays = [refs[i : i + 3] for i in (0, 3, 6)]
    outs = [refs[9 + i : 18 : 3] for i in range(3)]
    rings, sems = (refs[18:25], refs[25:32]), refs[32:36]
    factor = jnp.minimum(1.0, 0.5 * lax.rsqrt(squares[...] / (2 * 3 * ROWS * COLS) + 1e-30))[0:1, 0:1]
    steps = 2 * BLOCKS[0] + BLOCKS[1]

    def copies(kind, b, inward):
        down = kind == 2
        family = 1 if down else 0
        ring, cut, per = rings[family], CUTS[family], BLOCKS[family] // 2
        slot = lax.rem(b if down else b + kind * BLOCKS[0], DEPTH)
        layer, row = b // per, pl.multiple_of(lax.rem(b, per) * cut, cut)
        at = (layer, pl.ds(row, cut))
        if not inward:
            return [pltpu.make_async_copy(ring[4 + j].at[slot], outs[kind][j].at[at], sems[2 + family].at[slot * 3 + j]) for j in range(3)]
        first = pl.multiple_of((2 * kind + layer) * ROWS, ROWS)
        g = g_in.at[pl.ds(first, ROWS), pl.ds(row, cut)] if down else g_in.at[pl.ds(pl.multiple_of(first + row, cut), cut)]
        return [
            pltpu.make_async_copy(src, ring[j].at[slot], sems[family].at[slot * 4 + j])
            for j, src in enumerate((g, *(one.at[at] for one in arrays[kind])))
        ]

    def each(b, act):
        for kind in range(3):
            lo, hi = kind * BLOCKS[0], steps if kind == 2 else (kind + 1) * BLOCKS[0]
            pl.when(jnp.logical_and(b >= lo, b < hi))(lambda kind=kind, lo=lo: act(kind, b - lo))

    def start(kind, b):
        for copy in copies(kind, b, True):
            copy.start()

    def finish(kind, b):
        for copy in copies(kind, b, False):
            copy.wait()

    def step(kind, b):
        family = 1 if kind == 2 else 0
        ring = rings[family]
        slot = lax.rem(b if kind == 2 else b + kind * BLOCKS[0], DEPTH)
        for copy in copies(kind, b, True):
            copy.wait()
        g = ring[0][slot]
        g = (g.T if kind == 2 else g).astype(F32) * factor
        m = 0.9 * ring[2][slot] + 0.1 * g
        v = 0.95 * ring[3][slot] + 0.05 * g * g
        w = ring[1][slot].astype(F32)
        ring[4][slot] = (w - 0.02 * (m * lax.rsqrt(v + 1e-8) + 0.1 * w)).astype(BF)
        ring[5][slot] = m
        ring[6][slot] = v
        for copy in copies(kind, b, False):
            copy.start()

    for b in range(DEPTH):
        start(0, b)

    @pl.loop(0, steps)
    def _(b):
        pl.when(b >= DEPTH)(lambda: each(b - DEPTH, finish))
        each(b, step)
        each(b + DEPTH, start)

    pl.loop(steps - DEPTH, steps)(lambda b: each(b, finish))


def adamw(squares, summed, weights, m, v):
    any_ = pl.BlockSpec(memory_space=pl.ANY)
    dma, vmem = pltpu.SemaphoreType.DMA, pltpu.VMEM
    ring = lambda shape, turned: [vmem((DEPTH, *(turned or shape)), BF), vmem((DEPTH, *shape), BF)] + [vmem((DEPTH, *shape), F32)] * 2 + [
        vmem((DEPTH, *shape), BF)] + [vmem((DEPTH, *shape), F32)] * 2
    return pl.pallas_call(
        adamw_kernel,
        out_shape=[jax.ShapeDtypeStruct(w.shape, dtype) for dtype in (BF, F32, F32) for w in weights],
        in_specs=[pl.BlockSpec(memory_space=vmem)] + [any_] * 10,
        out_specs=[any_] * 9,
        scratch_shapes=ring((CUTS[0], COLS), None) + ring((CUTS[1], ROWS), (ROWS, CUTS[1]))
        + [dma((DEPTH * 4,)), dma((DEPTH * 4,)), dma((DEPTH * 3,)), dma((DEPTH * 3,))],
        compiler_params=pltpu.CompilerParams(vmem_limit_bytes=60 * 2**20),
        name="adamw",
    )(squares, summed, *(one for group in zip(weights, m, v, strict=True) for one in group))


MESH = pl.DeviceIdType.MESH
MATS = 6
HALF, QUARTER = ROWS // 2, ROWS // 4
N = MATS * TILES
SKEW = 2
LEAD = 2
LINE = 4
SLOTS = 8
PART = 256


def place(q):
    return lax.rem(lax.rem(q, 3) + 2, 3) * 2 + 1 - q // 3


def backward_kernel(*refs):
    dy_in, dyt_in, a0_in, a0t_in, p0_in, h1_in, a1t_in, p1_in, bg_in, bu_in, wg_in, wu_in, wd_in = refs[:13]
    out, squares_out, t, p, r, right, rows_g, rows_u, bg, bu, lhs0, lhs1, by_h, small, wg, wu, wd, acc, tile, sq = refs[13:33]
    load, right_sem, xs, xr, right_s, left_s, rs_r, ag_r, d_s, d_r, out_s, sq_s, sq_r = refs[33:]
    dp = lax.axis_index("dp")
    z, c = dp // 2, lax.rem(dp, 2)
    other = z * 2 + 1 - c

    def fetch(src, dst, n):
        return pltpu.make_async_copy(src, dst, load.at[n])

    get_dyt, get_a1t, get_dy, get_h1, get_wd0 = fetch(dyt_in, lhs0, 0), fetch(a1t_in, lhs1, 1), fetch(dy_in, by_h, 2), fetch(h1_in, small, 3), fetch(wd_in.at[0], wd, 4)
    get_wg1, get_wu1 = fetch(wg_in.at[1], wg, 5), fetch(wu_in.at[1], wu, 6)
    get_a0, get_wg0, get_wu0, get_a0t = fetch(a0_in, small, 7), fetch(wg_in.at[0], wg, 8), fetch(wu_in.at[0], wu, 9), fetch(a0t_in, lhs1, 10)

    def get_rows(i):
        at = pl.ds(pl.multiple_of(i * PART, PART), PART)
        return fetch(bg_in.at[at], rows_g, 11), fetch(bu_in.at[at], rows_u, 12)

    def get_right(k):
        at = pl.ds(pl.multiple_of(lax.rem(k, TILES) * TILE, TILE), TILE)
        slot = lax.rem(k, 2)
        return [pltpu.make_async_copy(src.at[:, at], right.at[slot], right_sem.at[slot]) for src in (p1_in, bg_in, bu_in, p0_in)]

    def start_right(k):
        for q, copy in enumerate(get_right(k)):
            pl.when(k // TILES == q)(copy.start)

    get_dyt.start()
    for k in range(2):
        start_right(jnp.int32(k))
    for copy in (get_a1t, get_dy, get_h1, get_wg1, get_wu1, get_wd0, *get_rows(0)):
        copy.start()
    barrier = pltpu.get_barrier_semaphore()
    for step in range(1, 8):
        pl.semaphore_signal(barrier, inc=1, device_id={"dp": lax.rem(dp + step, 8)}, device_id_type=MESH)
    pl.semaphore_wait(barrier, 7)
    acc[...] = jnp.zeros_like(acc)

    def exchange(k):
        return pltpu.make_async_remote_copy(
            src_ref=t.at[lax.rem(k, SLOTS), pl.ds(pl.multiple_of((1 - c) * HALF, 16), HALF)],
            dst_ref=p.at[k],
            send_sem=xs.at[k],
            recv_sem=xr.at[k],
            device_id={"dp": other},
            device_id_type=MESH,
        )

    def gradient(k):
        q, slot = k // TILES, lax.rem(k, SLOTS)

        @pl.when(k >= SLOTS)
        def _():
            exchange(k - SLOTS).wait_send()

        @pl.when(q < 4)
        def _():
            get_right(k)[0].wait()

        at = pl.ds(pl.multiple_of(lax.rem(k, TILES) * TILE, TILE), TILE)
        for which, left, operand in (
            (jnp.logical_or(q == 0, q == 3), lhs0, lambda: right[lax.rem(k, 2)]),
            (jnp.logical_or(q == 1, q == 2), lhs1, lambda: right[lax.rem(k, 2)]),
            (q == 4, lhs1, lambda: bg[:, at]),
            (q == 5, lhs1, lambda: bu[:, at]),
        ):
            @pl.when(which)
            def _(left=left, operand=operand):
                t[slot] = dot(left[...], operand()).astype(BF)

        exchange(k).start()
        pl.when(k + 2 < 4 * TILES)(lambda: start_right(k + 2))

    get_dyt.wait()
    for k in range(LEAD):
        gradient(jnp.int32(k))

    def through_layer(i):
        at = pl.ds(pl.multiple_of(i * PART, PART), PART)
        for copy in get_rows(i):
            copy.wait()
        by_a = dot_t(rows_g[...], wg[...]).astype(BF) + dot_t(rows_u[...], wu[...]).astype(BF)

        @pl.when(i + 1 < TOKENS // PART)
        def _():
            for copy in get_rows(i + 1):
                copy.start()

        by_a, wide_h = by_a.astype(F32), small[at, :].astype(F32)
        scale = lax.rsqrt(jnp.mean(wide_h * wide_h, -1, keepdims=True) + 1e-6)
        inner = jnp.mean(by_a * wide_h, -1, keepdims=True)
        by_h[at, :] = by_h[at, :] + (by_a * scale - wide_h * (scale * scale * scale * inner)).astype(BF)

    def first_layer(i):
        rows = pl.ds(pl.multiple_of(i // TILES * BLOCK, BLOCK), BLOCK)
        at = pl.ds(pl.multiple_of(lax.rem(i, TILES) * TILE, TILE), TILE)
        gate, up = dot(small[rows, :], wg[:, at]), dot(small[rows, :], wu[:, at])
        bg[rows, at], bu[rows, at], _ = by_gate_and_up(gate, up, dot_t(by_h[rows, :], wd[at, :]))

    parts, firsts = TOKENS // PART, TOKENS // BLOCK * TILES
    THROUGH = 2
    FIRST = THROUGH + parts + 1

    def work(i):
        @pl.when(i == THROUGH)
        def _():
            for copy in (get_wg1, get_wu1, get_h1, get_dy, get_a1t):
                copy.wait()

        @pl.when(jnp.logical_and(i >= THROUGH, i < THROUGH + parts))
        def _():
            through_layer(i - THROUGH)

        @pl.when(i == THROUGH + parts - 1)
        def _():
            for copy in (get_a0, get_wg0, get_wu0):
                copy.start()

        @pl.when(jnp.logical_and(i >= THROUGH + parts, i < THROUGH + 2 * parts))
        def _():
            at = pl.ds(pl.multiple_of((i - THROUGH - parts) * PART, PART), PART)
            lhs0[:, at] = by_h[at, :].T

        @pl.when(i == FIRST)
        def _():
            for copy in (get_a0, get_wg0, get_wu0, get_wd0):
                copy.wait()

        @pl.when(jnp.logical_and(i >= FIRST, i < FIRST + firsts // 2))
        def _():
            pl.loop(0, 2)(lambda n: first_layer((i - FIRST) * 2 + n))

        @pl.when(i == 4 * TILES - LEAD)
        def _():
            get_a0t.wait()

        pl.when(i + LEAD < N)(lambda: gradient(i + LEAD))

        @pl.when(i == 3 * TILES - LEAD)
        def _():
            get_a0t.start()

    def wide(k, x, core):
        rows = pl.ds(pl.multiple_of(place(k // TILES) * ROWS + core * HALF + x * QUARTER, 16), QUARTER)
        return rows, pl.ds(pl.multiple_of(lax.rem(k, TILES) * TILE, TILE), TILE)

    def narrow(k, x):
        return k, pl.ds(x * QUARTER, QUARTER)

    def term(k, x):
        return lax.rem(k, SLOTS), pl.ds(pl.multiple_of(c * HALF + x * QUARTER, 16), QUARTER)

    def sum_copy(k, x):
        return pltpu.make_async_remote_copy(
            src_ref=p.at[narrow(k, x)],
            dst_ref=r.at[narrow(k, x)],
            send_sem=right_s if x == 0 else left_s,
            recv_sem=rs_r.at[x * N + k],
            device_id={"dp": dp + 2 if x == 0 else dp - 2},
            device_id_type=MESH,
        )

    def back_copy(k, x, first=False):
        return pltpu.make_async_remote_copy(
            src_ref=r.at[narrow(k, x)] if first else out.at[wide(k, x, c)],
            dst_ref=out.at[wide(k, x, c)],
            send_sem=left_s if x == 0 else right_s,
            recv_sem=ag_r.at[x * N + k],
            device_id={"dp": dp - 2 if x == 0 else dp + 2},
            device_id_type=MESH,
        )

    def share_copy(k, x, first=False):
        return pltpu.make_async_remote_copy(
            src_ref=r.at[narrow(k, x)] if first else out.at[wide(k, x, c)],
            dst_ref=out.at[wide(k, x, c)],
            send_sem=d_s,
            recv_sem=d_r.at[x * N + k],
            device_id={"dp": other},
            device_id_type=MESH,
        )

    def share_arrival(k, x):
        return pltpu.make_async_remote_copy(
            src_ref=out.at[wide(k, x, 1 - c)],
            dst_ref=out.at[wide(k, x, 1 - c)],
            send_sem=d_s,
            recv_sem=d_r.at[x * N + k],
            device_id={"dp": other},
            device_id_type=MESH,
        )

    def valid(k):
        return jnp.logical_and(k >= 0, k < N)

    def add(k, x):
        hops = z if x == 0 else LINE - 1 - z

        first = z < LINE // 2 if x == 0 else z >= LINE // 2
        pl.when(first)(lambda: exchange(k).wait_recv())

        @pl.when(hops == 0)
        def _():
            mine = t[term(k, x)].astype(jnp.float32) + p[narrow(k, x)].astype(jnp.float32)
            p[narrow(k, x)] = mine.astype(jnp.bfloat16)
            sum_copy(k, x).start()

        @pl.when(hops > 0)
        def _():
            sum_copy(k, x).wait_recv()
            mine = t[term(k, x)].astype(jnp.float32) + p[narrow(k, x)].astype(jnp.float32)
            total = (mine + r[narrow(k, x)].astype(jnp.float32)).astype(jnp.bfloat16)

            @pl.when(hops < LINE - 1)
            def _():
                p[narrow(k, x)] = total
                sum_copy(k, x).start()

            @pl.when(hops == LINE - 1)
            def _():
                r[narrow(k, x)] = total
                back_copy(k, x, True).start()
                share_copy(k, x, True).start()
                pltpu.make_async_copy(r.at[narrow(k, x)], out.at[wide(k, x, c)], out_s).start()
                g = total.astype(jnp.float32)
                acc[...] += jnp.sum((g * g).reshape(QUARTER // 8, 8, TILE), axis=0)

    def relay(k, x):
        back_copy(k, x).wait_recv()

        @pl.when((z if x == 0 else LINE - 1 - z) > 0)
        def _():
            back_copy(k, x).start()

        share_copy(k, x).start()

    turn = SKEW * (LINE - 1)

    @pl.loop(0, N + 2 * turn + 1)
    def _(i):
        for x in range(2):
            k = i - SKEW * (z if x == 0 else LINE - 1 - z)
            pl.when(valid(k))(lambda k=k, x=x: add(k, x))
        for x in range(2):
            back = LINE - 1 - z if x == 0 else z
            k = i - turn - SKEW * back
            pl.when(jnp.logical_and(back > 0, valid(k)))(lambda k=k, x=x: relay(k, x))
            k = k - 1

            @pl.when(valid(k))
            def _(k=k, x=x):
                share_arrival(k, x).wait_recv()

        work(i)

    total = jnp.sum(acc[...])
    tile[...] = jnp.full(tile.shape, total, jnp.float32)

    def tell(slot, step):
        return pltpu.make_async_remote_copy(
            src_ref=tile, dst_ref=sq.at[slot], send_sem=sq_s.at[step - 1], recv_sem=sq_r.at[slot],
            device_id={"dp": lax.rem(dp + step, 8)}, device_id_type=MESH,
        )

    for slot, owner in enumerate((0, 1, 6, 7)):
        @pl.when(dp == owner)
        def _(slot=slot):
            for step in range(1, 8):
                tell(slot, step).start()
            sq[slot] = tile[...]

        @pl.when(dp != owner)
        def _(slot=slot):
            tell(slot, 1).wait_recv()

    squares_out[...] = sq[0] + sq[1] + sq[2] + sq[3]

    for slot, owner in enumerate((0, 1, 6, 7)):
        @pl.when(dp == owner)
        def _(slot=slot):
            for step in range(1, 8):
                tell(slot, step).wait_send()

    half = pl.ds(0, N // 2)

    def all_sent(sem):
        pltpu.make_async_remote_copy(src_ref=p, dst_ref=p, send_sem=sem, recv_sem=xr.at[0], device_id={"dp": other}, device_id_type=MESH).wait_send()

    pl.when(z < LINE - 1)(lambda: all_sent(right_s))
    pl.when(z > 0)(lambda: all_sent(left_s))
    all_sent(d_s)
    pl.loop(N - SLOTS, N)(lambda k: exchange(k).wait_send())

    @pl.when(jnp.logical_or(z == 0, z == LINE - 1))
    def _():
        pltpu.make_async_copy(r.at[half], p.at[half], out_s).wait()


def backward(arrays):
    dma = pltpu.SemaphoreType.DMA
    vmem = pltpu.VMEM
    return pl.pallas_call(
        backward_kernel,
        out_shape=(jax.ShapeDtypeStruct((MATS * ROWS, COLS), BF), jax.ShapeDtypeStruct((8, 128), F32)),
        in_specs=[pl.BlockSpec(memory_space=pl.ANY)] * len(arrays),
        out_specs=(pl.BlockSpec(memory_space=pl.ANY), pl.BlockSpec(memory_space=pltpu.VMEM)),
        scratch_shapes=[
            vmem((SLOTS, ROWS, TILE), BF),
            vmem((N, HALF, TILE), BF),
            vmem((N, HALF, TILE), BF),
            vmem((2, TOKENS, TILE), BF),
            vmem((PART, COLS), BF),
            vmem((PART, COLS), BF),
            vmem((TOKENS, COLS), BF),
            vmem((TOKENS, COLS), BF),
            vmem((ROWS, TOKENS), BF),
            vmem((ROWS, TOKENS), BF),
            vmem((TOKENS, ROWS), BF),
            vmem((TOKENS, ROWS), BF),
            vmem((ROWS, COLS), BF),
            vmem((ROWS, COLS), BF),
            vmem((COLS, ROWS), BF),
            vmem((8, TILE), F32),
            vmem((8, 128), F32),
            vmem((4, 8, 128), F32),
            dma((13,)), dma((2,)), dma((N,)), dma((N,)), dma(()), dma(()), dma((2 * N,)), dma((2 * N,)), dma(()), dma((2 * N,)), dma(()),
            dma((7,)), dma((4,)),
        ],
        compiler_params=pltpu.CompilerParams(collective_id=0, has_side_effects=True, vmem_limit_bytes=67043328),
        name="backward",
    )(*arrays)


def solution(mesh):
    def step(x, dy, *arrays):
        weights, m, v = (arrays[i : i + 3] for i in (0, 3, 6))
        x, dy = x[0], dy[0]
        kept = forward(x, dy, *weights)
        summed, squares = backward((dy, *kept, *weights))
        return tuple(adamw(squares, summed, weights, m, v))

    return jax.shard_map(
        step,
        mesh=mesh,
        in_specs=(P(("rep", "dp"), None, None),) * 2 + (P(None, None, None),) * 9,
        out_specs=(P("rep", None, None),) * 9,
        check_vma=False,
    )
```

time: 351 us -> 334 us (0.952)
  Pallas kernels: 350 us -> 333 us
    pallas_call x1, Pallas kernels: 231 us -> 219 us  [backward(): pl.pallas_call(backward_kernel, out_shape=(jax.ShapeDtypeStruct((MATS * R...]
    pallas_call x4 -> x2, Pallas kernels: 119 us -> 114 us  [the longest x1 60.6 us: adamw(): pl.pallas_call(adamw_kernel, out_shape=[jax.ShapeDtypeStruct(w.shape, dty...]
where the time goes in v3:
time: 334 us
  Pallas kernels  333 us (100%)
    pallas_call x1, Pallas kernels, backward(): pl.pallas_call(backward_kernel, out_shape=(jax.ShapeDtypeStruct((MATS * R...  219 us
    pallas_call x1, Pallas kernels, adamw(): pl.pallas_call(adamw_kernel, out_shape=[jax.ShapeDtypeStruct(w.shape, dty...  60.6 us
    pallas_call x1, Pallas kernels, forward(): pl.pallas_call(forward_kernel, grid=(TOKENS // BLOCK,), out_shape=(of_tur...  53.3 us

profile of v3, /device:TPU:0, one launch (start us, length us, event | category | flops | bytes accessed | tf_op | source)
XLA Modules:
  0.0 333.5 jit_solution(9523849260355225921)
XLA Ops:
  0.6 53.3 %forward.1 = (bf16[768,2048]{1,0:T(8,128)(2,1)}, bf16[2048,768]{1,0:T(8,128)(2,1)}, bf16[768,2048]{1,0:T(8,128)(2,1)}, bf16[2048,1792]{1,0:T(8,128)(2,1)}, bf16[...) custom-call(bf16[2048,768]{1,0:T(8,128)(2,1)} %bitcast.4, ...), custom_call_target="tpu_custom_call" | custom-call | tf_op jit(solution)/shard_map/forward/pallas_call | solution.py:87
  54.0 218.8 %backward.1 = (bf16[4608,1792]{1,0:T(8,128)(2,1)}, f32[8,128]{1,0:T(8,128)}) custom-call(bf16[2048,768]{1,0:T(8,128)(2,1)} %bitcast.3, bf16[768,2048]{1,0:T(8,128)(2,1)} %get-tuple-element.20.refs_1_, bf16[2048,768]{1,0:T(8,128)(2,1)} %get-tuple-element.21.refs_2_, bf16[768,2048]{1,0:T(8,128)(2,1)} %get-tuple-element.22.refs_3_, ...), custom_call_target="tpu_custom_call" | custom-call | tf_op jit(solution)/shard_map/backward/pallas_call | solution.py:503
  272.8 60.6 %adamw.1 = (bf16[2,768,1792]{2,1,0:T(8,128)(2,1)}, bf16[2,768,1792]{2,1,0:T(8,128)(2,1)}, bf16[2,1792,768]{2,1,0:T(8,128)(2,1)}, f32[2,768,1792]{2,1,0:T(8,128)}...) custom-call(f32[8,128]{1,0:T(8,128)} %get-tuple-element.29.squares, ...), custom_call_target="tpu_custom_call" | custom-call | tf_op jit(solution)/shard_map/adamw/pallas_call | solution.py:174

commit v4 on v3

--- a/solution.py
+++ b/solution.py
@@ -64,19 +64,31 @@
                 copies[i].wait()
 
     ready(0, 1)
-    for n in range(TILES):
-        at = slice(n * TILE, (n + 1) * TILE)
-        gate, up = dot(a0_out[...], weights[0][:, at]), dot(a0_out[...], weights[1][:, at])
-        p0_out[:, at] = (gate * sigmoid(gate) * up).astype(BF)
+    tiles = [slice(n * TILE, (n + 1) * TILE) for n in range(TILES)]
+
+    def pipelined(matmuls, rest):
+        last = None
+        for at in tiles:
+            now = matmuls(at)
+            if last is not None:
+                rest(*last)
+            last = at, now
+        rest(*last)
+
+    def product(at, two):
+        p0_out[:, at] = (two[0] * sigmoid(two[0]) * two[1]).astype(BF)
+
+    pipelined(lambda at: (dot(a0_out[...], weights[0][:, at]), dot(a0_out[...], weights[1][:, at])), product)
     ready(2)
     h1_out[...] = x[...] + dot(p0_out[...], weights[2][...]).astype(BF)
     a1[...] = normed(h1_out[...])
     a1t_out[...] = a1[...].T
     ready(3, 4, 5)
-    for n in range(TILES):
-        at = slice(n * TILE, (n + 1) * TILE)
-        gate, up = dot(a1[...], weights[3][:, at]), dot(a1[...], weights[4][:, at])
-        bg_out[:, at], bu_out[:, at], p1_out[:, at] = by_gate_and_up(gate, up, dot_t(dy[...], weights[5][at, :]))
+
+    def cotangents(at, three):
+        bg_out[:, at], bu_out[:, at], p1_out[:, at] = by_gate_and_up(*three)
+
+    pipelined(lambda at: (dot(a1[...], weights[3][:, at]), dot(a1[...], weights[4][:, at]), dot_t(dy[...], weights[5][at, :])), cotangents)
 
 
 def forward(x, dy, w_gate, w_up, w_down):
@@ -187,8 +199,10 @@
 MATS = 6
 HALF, QUARTER = ROWS // 2, ROWS // 4
 N = MATS * TILES
-SKEW = 2
+PIECES = 2 * N
+SKEW = 3
 LEAD = 2
+RING = 16
 LINE = 4
 SLOTS = 8
 PART = 256
@@ -200,11 +214,14 @@
 
 def backward_kernel(*refs):
     dy_in, dyt_in, a0_in, a0t_in, p0_in, h1_in, a1t_in, p1_in, bg_in, bu_in, wg_in, wu_in, wd_in = refs[:13]
-    out, squares_out, t, p, r, right, rows_g, rows_u, bg, bu, lhs0, lhs1, by_h, small, wg, wu, wd, acc, tile, sq = refs[13:33]
-    load, right_sem, xs, xr, right_s, left_s, rs_r, ag_r, d_s, d_r, out_s, sq_s, sq_r = refs[33:]
+    out, squares_out, t, p, done, arrived, swapped, right, rows_g, rows_u, bg, bu, lhs0, lhs1, by_h, small, wg, wu, wd, acc, tile, sq = refs[13:35]
+    load, right_sem, xs, xr, sent, got, swap_got, back_sent, d_s, d_r, out_s, sq_s, sq_r = refs[35:]
     dp = lax.axis_index("dp")
     z, c = dp // 2, lax.rem(dp, 2)
     other = z * 2 + 1 - c
+    outer = jnp.logical_or(z == 0, z == LINE - 1)
+    partner = lax.select(z < LINE // 2, 1 - z, 5 - z) * 2 + c
+    across = (LINE - 1 - z) * 2 + c
 
     def fetch(src, dst, n):
         return pltpu.make_async_copy(src, dst, load.at[n])
@@ -300,26 +317,29 @@
 
     parts, firsts = TOKENS // PART, TOKENS // BLOCK * TILES
     THROUGH = 2
-    FIRST = THROUGH + parts + 1
+    TURN = THROUGH + parts
+    FIRST = 2 * TURN + 2
 
     def work(i):
-        @pl.when(i == THROUGH)
+        turn, even = i // 2, lax.rem(i, 2) == 0
+
+        @pl.when(i == 2 * THROUGH)
         def _():
             for copy in (get_wg1, get_wu1, get_h1, get_dy, get_a1t):
                 copy.wait()
 
-        @pl.when(jnp.logical_and(i >= THROUGH, i < THROUGH + parts))
-        def _():
-            through_layer(i - THROUGH)
-
-        @pl.when(i == THROUGH + parts - 1)
+        @pl.when(jnp.logical_and(even, jnp.logical_and(turn >= THROUGH, turn < TURN)))
+        def _():
+            through_layer(turn - THROUGH)
+
+        @pl.when(i == 2 * TURN - 1)
         def _():
             for copy in (get_a0, get_wg0, get_wu0):
                 copy.start()
 
-        @pl.when(jnp.logical_and(i >= THROUGH + parts, i < THROUGH + 2 * parts))
-        def _():
-            at = pl.ds(pl.multiple_of((i - THROUGH - parts) * PART, PART), PART)
+        @pl.when(jnp.logical_and(even, jnp.logical_and(turn >= TURN, turn < TURN + parts)))
+        def _():
+            at = pl.ds(pl.multiple_of((turn - TURN) * PART, PART), PART)
             lhs0[:, at] = by_h[at, :].T
 
         @pl.when(i == FIRST)
@@ -327,130 +347,89 @@
             for copy in (get_a0, get_wg0, get_wu0, get_wd0):
                 copy.wait()
 
-        @pl.when(jnp.logical_and(i >= FIRST, i < FIRST + firsts // 2))
-        def _():
-            pl.loop(0, 2)(lambda n: first_layer((i - FIRST) * 2 + n))
-
-        @pl.when(i == 4 * TILES - LEAD)
+        @pl.when(jnp.logical_and(i >= FIRST, i < FIRST + firsts))
+        def _():
+            first_layer(i - FIRST)
+
+        @pl.when(i == 2 * (4 * TILES - LEAD))
         def _():
             get_a0t.wait()
 
-        pl.when(i + LEAD < N)(lambda: gradient(i + LEAD))
-
-        @pl.when(i == 3 * TILES - LEAD)
+        pl.when(jnp.logical_and(jnp.logical_not(even), turn + LEAD < N))(lambda: gradient(turn + LEAD))
+
+        @pl.when(i == 2 * (3 * TILES - LEAD))
         def _():
             get_a0t.start()
 
-    def wide(k, x, core):
-        rows = pl.ds(pl.multiple_of(place(k // TILES) * ROWS + core * HALF + x * QUARTER, 16), QUARTER)
+    def wide(h, core):
+        k = h // 2
+        rows = pl.ds(pl.multiple_of(place(k // TILES) * ROWS + core * HALF + lax.rem(h, 2) * QUARTER, 16), QUARTER)
         return rows, pl.ds(pl.multiple_of(lax.rem(k, TILES) * TILE, TILE), TILE)
 
-    def narrow(k, x):
-        return k, pl.ds(x * QUARTER, QUARTER)
-
-    def term(k, x):
-        return lax.rem(k, SLOTS), pl.ds(pl.multiple_of(c * HALF + x * QUARTER, 16), QUARTER)
-
-    def sum_copy(k, x):
+    def narrow(h):
+        return h // 2, pl.ds(pl.multiple_of(lax.rem(h, 2) * QUARTER, 16), QUARTER)
+
+    def remote(src, dst, send_sem, recv_sem, to):
         return pltpu.make_async_remote_copy(
-            src_ref=p.at[narrow(k, x)],
-            dst_ref=r.at[narrow(k, x)],
-            send_sem=right_s if x == 0 else left_s,
-            recv_sem=rs_r.at[x * N + k],
-            device_id={"dp": dp + 2 if x == 0 else dp - 2},
-            device_id_type=MESH,
+            src_ref=src, dst_ref=dst, send_sem=send_sem, recv_sem=recv_sem, device_id={"dp": to}, device_id_type=MESH
         )
 
-    def back_copy(k, x, first=False):
-        return pltpu.make_async_remote_copy(
-            src_ref=r.at[narrow(k, x)] if first else out.at[wide(k, x, c)],
-            dst_ref=out.at[wide(k, x, c)],
-            send_sem=left_s if x == 0 else right_s,
-            recv_sem=ag_r.at[x * N + k],
-            device_id={"dp": dp - 2 if x == 0 else dp + 2},
-            device_id_type=MESH,
-        )
-
-    def share_copy(k, x, first=False):
-        return pltpu.make_async_remote_copy(
-            src_ref=r.at[narrow(k, x)] if first else out.at[wide(k, x, c)],
-            dst_ref=out.at[wide(k, x, c)],
-            send_sem=d_s,
-            recv_sem=d_r.at[x * N + k],
-            device_id={"dp": other},
-            device_id_type=MESH,
-        )
-
-    def share_arrival(k, x):
-        return pltpu.make_async_remote_copy(
-            src_ref=out.at[wide(k, x, 1 - c)],
-            dst_ref=out.at[wide(k, x, 1 - c)],
-            send_sem=d_s,
-            recv_sem=d_r.at[x * N + k],
-            device_id={"dp": other},
-            device_id_type=MESH,
-        )
-
-    def valid(k):
-        return jnp.logical_and(k >= 0, k < N)
-
-    def add(k, x):
-        hops = z if x == 0 else LINE - 1 - z
-
-        first = z < LINE // 2 if x == 0 else z >= LINE // 2
-        pl.when(first)(lambda: exchange(k).wait_recv())
-
-        @pl.when(hops == 0)
-        def _():
-            mine = t[term(k, x)].astype(jnp.float32) + p[narrow(k, x)].astype(jnp.float32)
-            p[narrow(k, x)] = mine.astype(jnp.bfloat16)
-            sum_copy(k, x).start()
-
-        @pl.when(hops > 0)
-        def _():
-            sum_copy(k, x).wait_recv()
-            mine = t[term(k, x)].astype(jnp.float32) + p[narrow(k, x)].astype(jnp.float32)
-            total = (mine + r[narrow(k, x)].astype(jnp.float32)).astype(jnp.bfloat16)
-
-            @pl.when(hops < LINE - 1)
-            def _():
-                p[narrow(k, x)] = total
-                sum_copy(k, x).start()
-
-            @pl.when(hops == LINE - 1)
-            def _():
-                r[narrow(k, x)] = total
-                back_copy(k, x, True).start()
-                share_copy(k, x, True).start()
-                pltpu.make_async_copy(r.at[narrow(k, x)], out.at[wide(k, x, c)], out_s).start()
-                g = total.astype(jnp.float32)
-                acc[...] += jnp.sum((g * g).reshape(QUARTER // 8, 8, TILE), axis=0)
-
-    def relay(k, x):
-        back_copy(k, x).wait_recv()
-
-        @pl.when((z if x == 0 else LINE - 1 - z) > 0)
-        def _():
-            back_copy(k, x).start()
-
-        share_copy(k, x).start()
-
-    turn = SKEW * (LINE - 1)
-
-    @pl.loop(0, N + 2 * turn + 1)
+    def inward(h):
+        return remote(p.at[narrow(h)], arrived.at[lax.rem(h, RING)], sent, got.at[h], partner)
+
+    def swap(h):
+        return remote(p.at[narrow(h)], swapped.at[lax.rem(h, RING)], sent, swap_got.at[h], across)
+
+    def outward(h):
+        return remote(done.at[narrow(h)], out.at[wide(h, c)], back_sent, got.at[h], partner)
+
+    def share(h, first):
+        return remote(done.at[narrow(h)] if first else out.at[wide(h, c)], out.at[wide(h, c)], d_s, d_r, other)
+
+    def mine(h):
+        k = h // 2
+        pl.when(lax.rem(h, 2) == 0)(lambda: exchange(k).wait_recv())
+        own = t[lax.rem(k, SLOTS), pl.ds(pl.multiple_of(c * HALF + lax.rem(h, 2) * QUARTER, 16), QUARTER)]
+        return own.astype(F32) + p[narrow(h)].astype(F32)
+
+    def valid(h):
+        return jnp.logical_and(h >= 0, h < PIECES)
+
+    def send_in(h):
+        p[narrow(h)] = mine(h).astype(BF)
+        inward(h).start()
+
+    def add_and_swap(h):
+        total = mine(h)
+        inward(h).wait_recv()
+        p[narrow(h)] = (total + arrived[lax.rem(h, RING)].astype(F32)).astype(BF)
+        swap(h).start()
+
+    def finish(h):
+        swap(h).wait_recv()
+        g = (p[narrow(h)].astype(F32) + swapped[lax.rem(h, RING)].astype(F32)).astype(BF)
+        done[narrow(h)] = g
+        outward(h).start()
+        share(h, True).start()
+        pltpu.make_async_copy(done.at[narrow(h)], out.at[wide(h, c)], out_s).start()
+        g = g.astype(F32)
+        acc[...] += jnp.sum((g * g).reshape(QUARTER // 8, 8, TILE), axis=0)
+
+    def take(h):
+        outward(h).wait_recv()
+        share(h, False).start()
+
+    @pl.loop(0, PIECES + 3 * SKEW)
     def _(i):
-        for x in range(2):
-            k = i - SKEW * (z if x == 0 else LINE - 1 - z)
-            pl.when(valid(k))(lambda k=k, x=x: add(k, x))
-        for x in range(2):
-            back = LINE - 1 - z if x == 0 else z
-            k = i - turn - SKEW * back
-            pl.when(jnp.logical_and(back > 0, valid(k)))(lambda k=k, x=x: relay(k, x))
-            k = k - 1
-
-            @pl.when(valid(k))
-            def _(k=k, x=x):
-                share_arrival(k, x).wait_recv()
+        @pl.when(outer)
+        def _():
+            pl.when(valid(i - 3 * SKEW))(lambda: take(i - 3 * SKEW))
+            pl.when(valid(i))(lambda: send_in(i))
+
+        @pl.when(jnp.logical_not(outer))
+        def _():
+            pl.when(valid(i - 2 * SKEW))(lambda: finish(i - 2 * SKEW))
+            pl.when(valid(i - SKEW))(lambda: add_and_swap(i - SKEW))
 
         work(i)
 
@@ -463,7 +442,7 @@
             device_id={"dp": lax.rem(dp + step, 8)}, device_id_type=MESH,
         )
 
-    for slot, owner in enumerate((0, 1, 6, 7)):
+    for slot, owner in enumerate((2, 3)):
         @pl.when(dp == owner)
         def _(slot=slot):
             for step in range(1, 8):
@@ -474,27 +453,22 @@
         def _(slot=slot):
             tell(slot, 1).wait_recv()
 
-    squares_out[...] = sq[0] + sq[1] + sq[2] + sq[3]
-
-    for slot, owner in enumerate((0, 1, 6, 7)):
+    squares_out[...] = sq[0] + sq[1]
+
+    for slot, owner in enumerate((2, 3)):
         @pl.when(dp == owner)
         def _(slot=slot):
             for step in range(1, 8):
                 tell(slot, step).wait_send()
 
-    half = pl.ds(0, N // 2)
-
-    def all_sent(sem):
-        pltpu.make_async_remote_copy(src_ref=p, dst_ref=p, send_sem=sem, recv_sem=xr.at[0], device_id={"dp": other}, device_id_type=MESH).wait_send()
-
-    pl.when(z < LINE - 1)(lambda: all_sent(right_s))
-    pl.when(z > 0)(lambda: all_sent(left_s))
-    all_sent(d_s)
+    remote(p, p, sent, got.at[0], other).wait_send()
+    remote(p, p, d_s, d_r, other).wait()
     pl.loop(N - SLOTS, N)(lambda k: exchange(k).wait_send())
 
-    @pl.when(jnp.logical_or(z == 0, z == LINE - 1))
+    @pl.when(jnp.logical_not(outer))
     def _():
-        pltpu.make_async_copy(r.at[half], p.at[half], out_s).wait()
+        remote(p, p, back_sent, got.at[0], other).wait_send()
+        pltpu.make_async_copy(done, p, out_s).wait()
 
 
 def backward(arrays):
@@ -509,6 +483,8 @@
             vmem((SLOTS, ROWS, TILE), BF),
             vmem((N, HALF, TILE), BF),
             vmem((N, HALF, TILE), BF),
+            vmem((RING, QUARTER, TILE), BF),
+            vmem((RING, QUARTER, TILE), BF),
             vmem((2, TOKENS, TILE), BF),
             vmem((PART, COLS), BF),
             vmem((PART, COLS), BF),
@@ -523,9 +499,9 @@
             vmem((COLS, ROWS), BF),
             vmem((8, TILE), F32),
             vmem((8, 128), F32),
-            vmem((4, 8, 128), F32),
-            dma((13,)), dma((2,)), dma((N,)), dma((N,)), dma(()), dma(()), dma((2 * N,)), dma((2 * N,)), dma(()), dma((2 * N,)), dma(()),
-            dma((7,)), dma((4,)),
+            vmem((2, 8, 128), F32),
+            dma((13,)), dma((2,)), dma((N,)), dma((N,)), dma(()), dma((PIECES,)), dma((PIECES,)), dma(()), dma(()), dma(()), dma(()),
+            dma((7,)), dma((2,)),
         ],
         compiler_params=pltpu.CompilerParams(collective_id=0, has_side_effects=True, vmem_limit_bytes=67043328),
         name="backward",

time: 334 us -> 321 us (0.961)
  Pallas kernels: 333 us -> 320 us
    pallas_call x1, Pallas kernels: 219 us -> 206 us  [backward(): pl.pallas_call(backward_kernel, out_shape=(jax.ShapeDtypeStruct((MATS * R...]
where the time goes in v4:
time: 321 us; the launch traced here: 320 us
  Pallas kernels  320 us (100%)
    pallas_call x1, Pallas kernels, backward(): pl.pallas_call(backward_kernel, out_shape=(jax.ShapeDtypeStruct((MATS * R...  206 us
    pallas_call x1, Pallas kernels, adamw(): pl.pallas_call(adamw_kernel, out_shape=[jax.ShapeDtypeStruct(w.shape, dty...  60.6 us
    pallas_call x1, Pallas kernels, forward(): pl.pallas_call(forward_kernel, grid=(TOKENS // BLOCK,), out_shape=(of_tur...  53.4 us

profile of v4, /device:TPU:0, one launch (start us, length us, event | category | flops | bytes accessed | tf_op | source)
XLA Modules:
  0.0 320.5 jit_solution(10826343068160017990)
XLA Ops:
  0.6 53.4 %forward.1 = (bf16[768,2048]{1,0:T(8,128)(2,1)}, bf16[2048,768]{1,0:T(8,128)(2,1)}, bf16[768,2048]{1,0:T(8,128)(2,1)}, bf16[2048,1792]{1,0:T(8,128)(2,1)}, bf16[...) custom-call(bf16[2048,768]{1,0:T(8,128)(2,1)} %bitcast.4, ...), custom_call_target="tpu_custom_call" | custom-call | tf_op jit(solution)/shard_map/forward/pallas_call | solution.py:99
  54.0 205.7 %backward.1 = (bf16[4608,1792]{1,0:T(8,128)(2,1)}, f32[8,128]{1,0:T(8,128)}) custom-call(bf16[2048,768]{1,0:T(8,128)(2,1)} %bitcast.3, bf16[768,2048]{1,0:T(8,128)(2,1)} %get-tuple-element.20.refs_1_, bf16[2048,768]{1,0:T(8,128)(2,1)} %get-tuple-element.21.refs_2_, bf16[768,2048]{1,0:T(8,128)(2,1)} %get-tuple-element.22.refs_3_, ...), custom_call_target="tpu_custom_call" | custom-call | tf_op jit(solution)/shard_map/backward/pallas_call | solution.py:477
  259.8 60.6 %adamw.1 = (bf16[2,768,1792]{2,1,0:T(8,128)(2,1)}, bf16[2,768,1792]{2,1,0:T(8,128)(2,1)}, bf16[2,1792,768]{2,1,0:T(8,128)(2,1)}, f32[2,768,1792]{2,1,0:T(8,128)}...) custom-call(f32[8,128]{1,0:T(8,128)} %get-tuple-element.29.squares, ...), custom_call_target="tpu_custom_call" | custom-call | tf_op jit(solution)/shard_map/adamw/pallas_call | solution.py:186

commit v5 on v4

--- a/solution.py
+++ b/solution.py
@@ -41,7 +41,7 @@
 TILES = COLS // TILE
 
 
-def forward_kernel(x, dy, w_gate, w_up, w_down, dyt_out, a0_out, a0t_out, p0_out, h1_out, a1t_out, p1_out, bg_out, bu_out, *scratch):
+def forward_kernel(x, dy, w_gate, w_up, w_down, dyt_out, a0_out, p0_out, h1_out, a1t_out, p1_out, bg_out, bu_out, *scratch):
     weights, a1, sem = scratch[:6], scratch[6], scratch[7]
     copies = [pltpu.make_async_copy(w.at[n], weights[3 * n + i], sem.at[3 * n + i]) for n in range(2) for i, w in enumerate((w_gate, w_up, w_down))]
 
@@ -54,7 +54,6 @@
 
     a0 = normed(x[...])
     a0_out[...] = a0
-    a0t_out[...] = a0.T
     dyt_out[...] = dy[...].T
 
     def ready(*which):
@@ -99,17 +98,17 @@
     return pl.pallas_call(
         forward_kernel,
         grid=(TOKENS // BLOCK,),
-        out_shape=(of_turned, of(ROWS), of_turned, of(COLS), of(ROWS), of_turned, of(COLS), of(COLS), of(COLS)),
+        out_shape=(of_turned, of(ROWS), of(COLS), of(ROWS), of_turned, of(COLS), of(COLS), of(COLS)),
         in_specs=[narrow, narrow] + [pl.BlockSpec(memory_space=pl.ANY)] * 3,
-        out_specs=(turned, narrow, turned, wide, narrow, turned, wide, wide, wide),
+        out_specs=(turned, narrow, wide, narrow, turned, wide, wide, wide),
         scratch_shapes=[pltpu.VMEM(s, BF) for _ in range(2) for s in ((ROWS, COLS), (ROWS, COLS), (COLS, ROWS))] + [pltpu.VMEM((BLOCK, ROWS), BF), pltpu.SemaphoreType.DMA((6,))],
         compiler_params=pltpu.CompilerParams(vmem_limit_bytes=60 * 2**20),
         name="forward",
     )(x, dy, w_gate, w_up, w_down)
 
 
-DEPTH = 4
-CUTS = (128, 256)
+DEPTH = 8
+CUTS = (64, 128)
 BLOCKS = (2 * ROWS // CUTS[0], 2 * COLS // CUTS[1])
 
 
@@ -213,9 +212,9 @@
 
 
 def backward_kernel(*refs):
-    dy_in, dyt_in, a0_in, a0t_in, p0_in, h1_in, a1t_in, p1_in, bg_in, bu_in, wg_in, wu_in, wd_in = refs[:13]
-    out, squares_out, t, p, done, arrived, swapped, right, rows_g, rows_u, bg, bu, lhs0, lhs1, by_h, small, wg, wu, wd, acc, tile, sq = refs[13:35]
-    load, right_sem, xs, xr, sent, got, swap_got, back_sent, d_s, d_r, out_s, sq_s, sq_r = refs[35:]
+    dy_in, dyt_in, a0_in, p0_in, h1_in, a1t_in, p1_in, bg_in, bu_in, wg_in, wu_in, wd_in = refs[:12]
+    out, squares_out, t, p, done, arrived, swapped, right, rows_g, rows_u, bg, bu, lhs0, lhs1, by_h, small, wg, wu, wd, acc, tile, sq = refs[12:34]
+    load, right_sem, xs, xr, sent, got, swap_got, back_sent, d_s, d_r, out_s, sq_s, sq_r = refs[34:]
     dp = lax.axis_index("dp")
     z, c = dp // 2, lax.rem(dp, 2)
     other = z * 2 + 1 - c
@@ -228,11 +227,11 @@
 
     get_dyt, get_a1t, get_dy, get_h1, get_wd0 = fetch(dyt_in, lhs0, 0), fetch(a1t_in, lhs1, 1), fetch(dy_in, by_h, 2), fetch(h1_in, small, 3), fetch(wd_in.at[0], wd, 4)
     get_wg1, get_wu1 = fetch(wg_in.at[1], wg, 5), fetch(wu_in.at[1], wu, 6)
-    get_a0, get_wg0, get_wu0, get_a0t = fetch(a0_in, small, 7), fetch(wg_in.at[0], wg, 8), fetch(wu_in.at[0], wu, 9), fetch(a0t_in, lhs1, 10)
+    get_a0, get_wg0, get_wu0 = fetch(a0_in, small, 7), fetch(wg_in.at[0], wg, 8), fetch(wu_in.at[0], wu, 9)
 
     def get_rows(i):
         at = pl.ds(pl.multiple_of(i * PART, PART), PART)
-        return fetch(bg_in.at[at], rows_g, 11), fetch(bu_in.at[at], rows_u, 12)
+        return fetch(bg_in.at[at], rows_g, 10), fetch(bu_in.at[at], rows_u, 11)
 
     def get_right(k):
         at = pl.ds(pl.multiple_of(lax.rem(k, TILES) * TILE, TILE), TILE)
@@ -319,6 +318,7 @@
     THROUGH = 2
     TURN = THROUGH + parts
     FIRST = 2 * TURN + 2
+    AGAIN = 2 * (3 * TILES - LEAD)
 
     def work(i):
         turn, even = i // 2, lax.rem(i, 2) == 0
@@ -351,15 +351,12 @@
         def _():
             first_layer(i - FIRST)
 
-        @pl.when(i == 2 * (4 * TILES - LEAD))
-        def _():
-            get_a0t.wait()
-
         pl.when(jnp.logical_and(jnp.logical_not(even), turn + LEAD < N))(lambda: gradient(turn + LEAD))
 
-        @pl.when(i == 2 * (3 * TILES - LEAD))
-        def _():
-            get_a0t.start()
+        @pl.when(jnp.logical_and(i >= AGAIN, i < AGAIN + parts))
+        def _():
+            at = pl.ds(pl.multiple_of((i - AGAIN) * PART, PART), PART)
+            lhs1[:, at] = small[at, :].T
 
     def wide(h, core):
         k = h // 2
@@ -500,7 +497,7 @@
             vmem((8, TILE), F32),
             vmem((8, 128), F32),
             vmem((2, 8, 128), F32),
-            dma((13,)), dma((2,)), dma((N,)), dma((N,)), dma(()), dma((PIECES,)), dma((PIECES,)), dma(()), dma(()), dma(()), dma(()),
+            dma((12,)), dma((2,)), dma((N,)), dma((N,)), dma(()), dma((PIECES,)), dma((PIECES,)), dma(()), dma(()), dma(()), dma(()),
             dma((7,)), dma((2,)),
         ],
         compiler_params=pltpu.CompilerParams(collective_id=0, has_side_effects=True, vmem_limit_bytes=67043328),

time: 321 us -> 318 us (level)
  no operation moved by 1% of the time
where the time goes in v5:
time: 318 us
  Pallas kernels  317 us (100%)
    pallas_call x1, Pallas kernels, backward(): pl.pallas_call(backward_kernel, out_shape=(jax.ShapeDtypeStruct((MATS * R...  206 us
    pallas_call x1, Pallas kernels, adamw(): pl.pallas_call(adamw_kernel, out_shape=[jax.ShapeDtypeStruct(w.shape, dty...  59.4 us
    pallas_call x1, Pallas kernels, forward(): pl.pallas_call(forward_kernel, grid=(TOKENS // BLOCK,), out_shape=(of_tur...  52 us

profile of v5, /device:TPU:0, one launch (start us, length us, event | category | flops | bytes accessed | tf_op | source)
XLA Modules:
  0.0 318.0 jit_solution(5943411334172875100)
XLA Ops:
  0.6 52.0 %forward.1 = (bf16[768,2048]{1,0:T(8,128)(2,1)}, bf16[2048,768]{1,0:T(8,128)(2,1)}, bf16[2048,1792]{1,0:T(8,128)(2,1)}, bf16[2048,768]{1,0:T(8,128)(2,1)}, bf16[...) custom-call(bf16[2048,768]{1,0:T(8,128)(2,1)} %bitcast.4, ...), custom_call_target="tpu_custom_call" | custom-call | tf_op jit(solution)/shard_map/forward/pallas_call | solution.py:98
  52.7 205.8 %backward.1 = (bf16[4608,1792]{1,0:T(8,128)(2,1)}, f32[8,128]{1,0:T(8,128)}) custom-call(bf16[2048,768]{1,0:T(8,128)(2,1)} %bitcast.3, bf16[768,2048]{1,0:T(8,128)(2,1)} %get-tuple-element.19.refs_1_, bf16[2048,768]{1,0:T(8,128)(2,1)} %get-tuple-element.20.refs_2_, bf16[2048,1792]{1,0:T(8,128)(2,1)} %get-tuple-element.21.refs_3_, ...), custom_call_target="tpu_custom_call" | custom-call | tf_op jit(solution)/shard_map/backward/pallas_call | solution.py:474
  258.4 59.4 %adamw.1 = (bf16[2,768,1792]{2,1,0:T(8,128)(2,1)}, bf16[2,768,1792]{2,1,0:T(8,128)(2,1)}, bf16[2,1792,768]{2,1,0:T(8,128)(2,1)}, f32[2,768,1792]{2,1,0:T(8,128)}...) custom-call(f32[8,128]{1,0:T(8,128)} %get-tuple-element.27.squares, ...), custom_call_target="tpu_custom_call" | custom-call | tf_op jit(solution)/shard_map/adamw/pallas_call | solution.py:185
